TPU v7x, 32 devices: a whole 2x2x4 slice. The times are simulated.
32 devices in a mesh: member: 2 (over core), section: 4 (over y, x), atoms: 4 (over z).
Axes of the slice: x: 2, y: 2, z: 4, core: 2. Of those that a mesh axis runs over, the one named last changes fastest.
Arguments:
- positions: float32 [8, 3, 512], P(None, None, 'atoms'), may hold values from -8 to 8
- atom_types: int32 [8, 512], P(None, 'atoms'), may hold values from 0 to 127
- neighbors: int32 [8, 512, 128], P(None, 'atoms'), may hold values from 0 to 511
- nbr_mask: int32 [8, 512, 128], P(None, 'atoms'), may hold values 0 or 1
- type_table: bfloat16 [2, 128, 128], P('member'), may hold values from -6 to 6
- norm_gain: bfloat16 [2, 4, 128], P('member', 'section'), may hold values from 0.25 to 1.75
- proj_weight: bfloat16 [2, 4, 128, 384], P('member', 'section'), may hold values from -0.5 to 0.5
- out_weight: bfloat16 [2, 4, 128, 128], P('member', 'section'), may hold values from -0.5 to 0.5
- force_coef: bfloat16 [2, 4, 4], P('member', 'section'), may hold values from -48 to 48
Outputs:
- atom_dev: float32 [8, 512], P('section', 'atoms')
- max_dev: float32 [8], P('section')
- mean_force: float32 [8, 3, 512], P('section', None, 'atoms')
Inputs may be any that keep to these rules, and one draw needn't show every extreme that they name: `neighbors`: indices of atoms of the same frame, repeats and the atom itself allowed.
All inputs are finite; a program needn't handle non-finite values. No bound on the sum of `nbr_mask` on one device may be relied on, other than what follows from the above.
Results may differ from a plain program's by a relative error of at most 0.013.
Values may be sent and summed in bfloat16 or wider, within the bound.
No kernel may reach another device: no remote copies, remote signals or barrier semaphores. Data moves between devices by JAX's collectives and lax.ppermute only.
A program may use at most 64 MiB of HBM per device.

v0:
```python
import math

import jax
import jax.numpy as jnp
from jax import lax
from jax.experimental import pallas as pl
from jax.experimental.pallas import tpu as pltpu
from jax.sharding import PartitionSpec as P

F32 = jnp.float32
BF16 = jnp.bfloat16
EXTRA = 8
NIBBLES = 8
AHEAD = 6
LAG = 2
WROWS = 16
FRAME_PARAMS = pltpu.CompilerParams(vmem_limit_bytes=32 << 20)
SMALL_PARAMS = pltpu.CompilerParams(vmem_limit_bytes=8 << 20)


def dest(axis_size, index, r):
    if axis_size & (axis_size - 1) == 0:
        return index ^ r
    return (index + r) % axis_size


def source(axis_size, index, r):
    if axis_size & (axis_size - 1) == 0:
        return index ^ r
    return (index - r) % axis_size


def exchange(x, axis, axis_size, r):
    if r == 0:
        return x
    return lax.ppermute(x, axis, [(i, dest(axis_size, i, r)) for i in range(axis_size)])


def dot(a, b):
    return lax.dot_general(a, b, (((1,), (0,)), ((), ())), preferred_element_type=F32)


def pack_kernel(n_section, pos_ref, typ_ref, nbr_ref, mask_ref, proj_ref, outw_ref, *refs):
    gain_ref, coef_ref = refs[:2]
    frames = pos_ref.shape[1]
    per_section = frames // n_section
    outs, w_out = refs[2 : 2 + per_section], refs[2 + per_section]
    pos_v, typ_v, nbr_v, mask_v, gain_v, coef_v, sems = refs[3 + per_section :]
    first = lax.axis_index("section") * per_section
    mine = lax.axis_index("atoms") % per_section
    side = outw_ref.shape[0]
    small = [
        pltpu.make_async_copy(pos_ref, pos_v, sems.at[0]),
        pltpu.make_async_copy(typ_ref, typ_v, sems.at[1]),
    ]
    for c in small:
        c.start()
    lists = []
    for x in range(per_section):
        frame = first + dest(per_section, mine, x)
        a = pltpu.make_async_copy(nbr_ref.at[frame], nbr_v.at[x], sems.at[6 + 2 * x])
        b = pltpu.make_async_copy(mask_ref.at[frame], mask_v.at[x], sems.at[7 + 2 * x])
        a.start()
        b.start()
        lists.append((frame, a, b))
    weights = [
        pltpu.make_async_copy(proj_ref, w_out.at[:side, : 3 * side], sems.at[2]),
        pltpu.make_async_copy(outw_ref, w_out.at[:side, 3 * side :], sems.at[3]),
        pltpu.make_async_copy(gain_ref, gain_v, sems.at[4]),
        pltpu.make_async_copy(coef_ref, coef_v, sems.at[5]),
    ]
    for c in weights:
        c.start()
    for c in small:
        c.wait()
    for x, (frame, a, b) in enumerate(lists):
        a.wait()
        b.wait()
        slots = nbr_v.shape[2]
        count = nbr_v.shape[1]
        eff = jnp.where(mask_v[x] != 0, nbr_v[x], -1).astype(F32)
        outs[x][:slots, :] = jnp.transpose(eff)
        rows = [pos_v[c, pl.ds(frame, 1), :] for c in range(3)]
        rows.append(typ_v[pl.ds(frame, 1), :].astype(F32))
        rows.append(jnp.zeros((EXTRA - 4, count), F32))
        outs[x][slots:, :] = jnp.concatenate(rows, axis=0)
    for c in weights:
        c.wait()
    heads = coef_v.shape[1]
    row = jnp.concatenate(
        [gain_v[...], coef_v[...], jnp.zeros((1, 3 * side - heads), BF16)], axis=1
    )
    w_out[side:, :] = jnp.broadcast_to(row.astype(F32), (WROWS, 4 * side)).astype(BF16)


def count_slots(list_ref, slots, total, cnt_ref):
    count = list_ref.shape[1]
    low = total // NIBBLES
    iota = lax.broadcasted_iota(jnp.int32, (low, count), 0)
    cnt_ref[...] = jnp.zeros_like(cnt_ref)

    def chunk(c, carry):
        eff = list_ref[pl.ds(c * 8, 8), :]
        hi = jnp.floor((eff + 0.5) * (1.0 / low))
        lo = jnp.where(eff < 0, -1.0, eff - hi * low).astype(jnp.int32)
        weight = jnp.left_shift(1, 4 * jnp.maximum(hi, 0.0).astype(jnp.int32))
        nib = None
        for s in range(8):
            one = jnp.where(iota == lo[s : s + 1, :], weight[s : s + 1, :], 0)
            nib = one if nib is None else nib + one
        cnt_ref[:low, :] += nib & 0x0F0F0F0F
        cnt_ref[low:, :] += lax.shift_right_logical(nib, 4) & 0x0F0F0F0F
        return carry

    lax.fori_loop(0, slots // 8, chunk, 0)


def slice_kernel(total, msg_ref, cnt_ref):
    count_slots(msg_ref, msg_ref.shape[0] - EXTRA, total, cnt_ref)


def frame_kernel(n_section, n_atoms, heads, slots, *refs):
    msgs, refs = refs[:n_atoms], refs[n_atoms:]
    weights_in, refs = refs[:n_section], refs[n_section:]
    cnt_v, refs = refs[:n_atoms], refs[n_atoms:]
    table_ref, out_ref, ext_v, w_v, p_v = refs
    count = msgs[0].shape[1]
    total = n_atoms * count
    width = table_ref.shape[1]
    head_dim = width // heads
    low = total // NIBBLES
    a_idx = lax.axis_index("atoms")
    s_idx = lax.axis_index("section")
    tile = max(count, min(256, total // 4))
    tiles = total // tile
    per_tile = tile // count
    group = max(1, 256 // tile)
    span = [slice(t * tile, (t + 1) * tile) for t in range(tiles)]

    for r in range(n_section):
        w = weights_in[r][...]
        side = w.shape[0] - WROWS
        gain = jnp.transpose(
            jnp.broadcast_to(w[side : side + 1, :side].astype(F32), (side, side))
        ).astype(BF16)
        w_v[source(n_section, s_idx, r)] = jnp.concatenate(
            [jnp.transpose(w[:side]), gain, w[side:, :side], w[side:, side : 2 * side]], axis=0
        )

    ext = [msgs[r][slots:, :] for r in range(n_atoms)]
    for r in range(n_atoms):
        ext_v[source(n_atoms, a_idx, r)] = ext[r]
    pos_col = jnp.concatenate([jnp.transpose(ext_v[b]) for b in range(n_atoms)], axis=0)
    pos = jnp.concatenate(ext, axis=1)[:3]
    pos_hi = pos.astype(BF16).astype(F32)
    tail = jnp.concatenate(
        [pos_hi, pos - pos_hi, jnp.ones((1, total), F32), jnp.zeros((9, total), F32)], axis=0
    ).astype(BF16)
    types = jnp.concatenate(ext, axis=1)[3:4].astype(jnp.int32)
    iota_t = lax.broadcasted_iota(jnp.int32, (table_ref.shape[0], total), 0)
    onehot = (iota_t == types).astype(BF16)
    embed = dot(jnp.transpose(table_ref[...]), onehot)

    def pairs(r):
        lanes = slice(r * count, (r + 1) * count)
        for n in range(NIBBLES):
            acc = cnt_v[r][low:, :] if n % 2 else cnt_v[r][:low, :]
            hits = (lax.shift_right_logical(acc, 8 * (n // 2)) & 0xFF).astype(F32)
            part = pos_col[n * low : (n + 1) * low]
            dist = None
            for c in range(3):
                delta = part[:, c : c + 1] - ext[r][c : c + 1, :]
                dist = delta * delta if dist is None else dist + delta * delta
            p_v[n * low : (n + 1) * low, lanes] = 0.5 * hits / (1.0 + 0.125 * dist)

    scale = 0.5 / math.sqrt(head_dim)
    h = [embed[:, span[t]] for t in range(tiles)]
    state = {}
    force = [None] * tiles
    results = {}
    zeros = {}

    def zero_rows(n):
        if n not in zeros:
            zeros[n] = jnp.zeros((n, tile), BF16)
        return zeros[n]

    def project(b, t):
        w = w_v[b]
        norm = lax.rsqrt(jnp.mean(h[t] * h[t], axis=0, keepdims=True) + 1e-06)
        x = (h[t] * norm * w[4 * width : 5 * width, :1].astype(F32)).astype(BF16)
        qkv = dot(w[: 3 * width, :width], x)
        k = jnp.transpose(qkv[width : 2 * width].astype(BF16))
        q = (qkv[:width] * scale).astype(BF16)
        v = qkv[2 * width :].astype(BF16)
        rhs = []
        for first in range(0, heads, group):
            cols = []
            for hd in range(first, first + group):
                rows = [q[hd * head_dim : (hd + 1) * head_dim]]
                if hd > 0:
                    rows.insert(0, zero_rows(hd * head_dim))
                if hd < heads - 1:
                    rows.append(zero_rows((heads - 1 - hd) * head_dim))
                cols.append(jnp.concatenate(rows, axis=0))
            rhs.append(jnp.concatenate(cols, axis=1))
        state[b, t] = rhs, k, v

    def score(b, t, jt, g):
        return dot(state[b, jt][1], state[b, t][0][g])

    def consume(unit, value):
        _, t, jt, _ = unit
        p = jnp.concatenate(
            [
                p_v[pl.ds(source(n_atoms, a_idx, r) * count, count), span[t]]
                for r in range(jt * per_tile, (jt + 1) * per_tile)
            ],
            axis=0,
        )
        parts = []
        for i in range(group):
            parts.append(p * jnp.tanh(value[:, i * tile : (i + 1) * tile]) + p)
        return jnp.concatenate(parts, axis=1).astype(BF16)

    def message(unit, value):
        b, t, jt, g = unit
        rows = slice(g * group * head_dim, (g + 1) * group * head_dim)
        lhs = jnp.concatenate([state[b, jt][2][rows], tail[:, span[jt]]], axis=0)
        res = dot(lhs, value)
        for i in range(group):
            lanes = slice(i * tile, (i + 1) * tile)
            own = (
                res[i * head_dim : (i + 1) * head_dim, lanes],
                res[group * head_dim : group * head_dim + 8, lanes],
            )
            key = b, t, g * group + i
            if key in results:
                own = tuple(x + y for x, y in zip(results[key], own))
            results[key] = own

    def finish(b, t):
        w = w_v[b]
        parts = [results.pop((b, t, hd)) for hd in range(heads)]
        if b + 1 < n_section:
            msg = jnp.concatenate([part[0] for part in parts], axis=0) * (1.0 / slots)
            step = dot(w[3 * width : 4 * width], msg.astype(BF16))
            h[t] = (h[t] + step).astype(BF16).astype(F32)
            project(b + 1, t)
        coef = w[5 * width + WROWS : 5 * width + WROWS + 1, :heads].astype(F32)
        for hd, part in enumerate(parts):
            term = coef[:, hd : hd + 1] * part[1]
            force[t] = term if force[t] is None else force[t] + term

    last = tiles - 1
    order = [(t, jt) for t in range(last) for jt in range(last)]
    order += [(t, last) for t in range(last)]
    order += [(last, jt) for jt in range(tiles)]
    units = [
        (b, t, jt, g) for b in range(n_section) for t, jt in order for g in range(heads // group)
    ]
    left = {(b, t): tiles * (heads // group) for b in range(n_section) for t in range(tiles)}
    ready = set()
    pending, gated = [], []

    def retire():
        if pending:
            gate()
        if len(gated) > LAG or not pending:
            settle()

    def settle():
        unit, value = gated.pop(0)
        b, t = unit[:2]
        message(unit, value)
        left[b, t] -= 1
        if left[b, t] == 0:
            finish(b, t)

    def gate():
        unit, value = pending.pop(0)
        _, t = unit[:2]
        for r in range(t * per_tile, (t + 1) * per_tile):
            if r not in ready:
                ready.add(r)
                pairs(r)
        gated.append((unit, consume(unit, value)))

    for t in range(tiles):
        project(0, t)
    for unit in units:
        b, t, jt, _ = unit
        while (b, t) not in state or (b, jt) not in state:
            retire()
        pending.append((unit, score(*unit)))
        while len(pending) > AHEAD:
            retire()
    while pending or gated:
        retire()

    f = jnp.concatenate(force, axis=1)
    out = (f[0:3] + f[3:6] - pos * f[6:7]) * (1.0 / slots)
    out_ref[...] = jnp.concatenate([out, jnp.zeros((5, total), F32)], axis=0)


def emit_kernel(n_member, n_atoms, count, *refs):
    ins, (dev_ref, max_ref, mean_ref, members_v) = refs[:-4], refs[-4:]
    per_section = len(ins) // n_member
    mine = lax.axis_index("atoms") % per_section
    own = lax.axis_index("member")
    for x in range(per_section):
        for r in range(n_member):
            members_v[source(n_member, own, r)] = ins[x * n_member + r][...]
        forces = [members_v[m][:3] for m in range(n_member)]
        mean = sum(forces) * (1.0 / n_member)
        spread = sum(jnp.sum((f - mean) * (f - mean), 0, keepdims=True) for f in forces)
        dev = jnp.sqrt(spread * (1.0 / n_member))
        r = x if n_atoms & (n_atoms - 1) == 0 else (-x) % n_atoms
        lanes = slice(r * count, (r + 1) * count)
        frame = source(per_section, mine, x)
        dev_ref[pl.ds(frame, 1), :] = dev[:, lanes]
        for c in range(3):
            mean_ref[c, pl.ds(frame, 1), :] = mean[c : c + 1, lanes]
        max_ref[frame] = jnp.max(dev)


def shards(n_member, n_section, n_atoms):
    def body(
        positions,
        atom_types,
        neighbors,
        nbr_mask,
        type_table,
        norm_gain,
        proj_weight,
        out_weight,
        force_coef,
    ):
        frames = positions.shape[0]
        per_section = frames // n_section
        count, slots = neighbors.shape[1:]
        total = count * n_atoms
        heads = force_coef.shape[-1]
        width = out_weight.shape[-1]
        any_spec = pl.BlockSpec(memory_space=pl.ANY)
        vmem = pl.BlockSpec(memory_space=pltpu.VMEM)
        smem = pl.BlockSpec(memory_space=pltpu.SMEM)
        shape = jax.ShapeDtypeStruct

        *packed, own_w = pl.pallas_call(
            lambda *refs: pack_kernel(n_section, *refs),
            out_shape=[shape((slots + EXTRA, count), F32)] * per_section
            + [shape((width + WROWS, 4 * width), BF16)],
            in_specs=[any_spec] * 8,
            out_specs=[vmem] * (per_section + 1),
            scratch_shapes=[
                pltpu.VMEM((3, frames, count), F32),
                pltpu.VMEM((frames, count), jnp.int32),
                pltpu.VMEM((per_section, count, slots), jnp.int32),
                pltpu.VMEM((per_section, count, slots), jnp.int32),
                pltpu.VMEM((1, width), BF16),
                pltpu.VMEM((1, heads), BF16),
                pltpu.SemaphoreType.DMA((6 + 2 * per_section,)),
            ],
            compiler_params=SMALL_PARAMS,
            name="pack",
        )(
            *[
                pltpu.with_memory_space_constraint(x, pltpu.HBM)
                for x in (
                    jnp.transpose(positions, (1, 0, 2)),
                    atom_types,
                    neighbors,
                    nbr_mask,
                    proj_weight[0, 0],
                    out_weight[0, 0],
                    norm_gain[0],
                    force_coef[0],
                )
            ]
        )
        lists = [exchange(packed[r % per_section], "atoms", n_atoms, r) for r in range(n_atoms)]
        weights = [exchange(own_w, "section", n_section, r) for r in range(n_section)]

        low = total // NIBBLES
        counted = [
            pl.pallas_call(
                lambda *refs: slice_kernel(total, *refs),
                out_shape=shape((2 * low, count), jnp.int32),
                in_specs=[vmem],
                out_specs=vmem,
                compiler_params=SMALL_PARAMS,
                name="slice",
            )(msg)
            for msg in lists
        ]
        force = pl.pallas_call(
            lambda *refs: frame_kernel(n_section, n_atoms, heads, slots, *refs),
            out_shape=shape((8, total), F32),
            in_specs=[vmem] * (2 * n_atoms + n_section + 1),
            out_specs=vmem,
            scratch_shapes=[
                pltpu.VMEM((n_atoms, EXTRA, count), F32),
                pltpu.VMEM((n_section, 5 * width + 2 * WROWS, width), BF16),
                pltpu.VMEM((total, total), F32),
            ],
            compiler_params=FRAME_PARAMS,
            name="frame",
        )(*lists, *weights, *counted, type_table[0])

        def joint(x, r):
            if x == 0 and r == 0:
                return force
            pairs = [
                (m * n_atoms + a, dest(n_member, m, r) * n_atoms + dest(n_atoms, a, x))
                for m in range(n_member)
                for a in range(n_atoms)
            ]
            return lax.ppermute(force, ("member", "atoms"), pairs)

        got = [joint(x, r) for x in range(per_section) for r in range(n_member)]
        atom_dev, max_dev, mean_force = pl.pallas_call(
            lambda *refs: emit_kernel(n_member, n_atoms, count, *refs),
            out_shape=[
                shape((per_section, count), F32),
                shape((per_section,), F32),
                shape((3, per_section, count), F32),
            ],
            in_specs=[vmem] * len(got),
            out_specs=[vmem, smem, vmem],
            scratch_shapes=[pltpu.VMEM((n_member, 8, total), F32)],
            compiler_params=SMALL_PARAMS,
            name="emit",
        )(*got)
        return atom_dev, max_dev, jnp.transpose(mean_force, (1, 0, 2))

    return body


def solution(mesh):
    sizes = mesh.shape
    return jax.shard_map(
        shards(sizes["member"], sizes["section"], sizes["atoms"]),
        mesh=mesh,
        in_specs=(
            P(None, None, "atoms"),
            P(None, "atoms"),
            P(None, "atoms", None),
            P(None, "atoms", None),
            P("member", None, None),
            P("member", "section", None),
            P("member", "section", None, None),
            P("member", "section", None, None),
            P("member", "section", None),
        ),
        out_specs=(P("section", "atoms"), P("section"), P("section", None, "atoms")),
        check_vma=False,
    )
```

profile of v0, /device:TPU:0, one launch (start us, length us, event | category | flops | bytes accessed | tf_op | source)
XLA Modules:
  0.0 31.2 jit_solution(5713478309437618342)
XLA Ops:
  0.6 1.2 %pack.1 = (f32[136,128]{1,0:T(8,128)S(1)}, f32[136,128]{1,0:T(8,128)S(1)}, bf16[144,512]{1,0:T(8,128)(2,1)S(1)}) custom-call(f32[3,8,128]{2,1,0:T(8,128)} %bitcast.10, s32[8,128]{1,0:T(8,128)} %refs_1_.1, s32[8,128,128]{2,1,0:T(8,128)} %refs_2_.1, s32[8,128,128]{2,1,0:T(8,128)} %refs_3_.1, bf16[128,384]{1,0:T(8,128)(2,1)} %bitcast.8, ...), custom_call_target="tpu_custom_call" | custom-call | tf_op jit(solution)/shard_map/pack/pallas_call | solution.py:350
  1.9 4.0 %collective-permute-start.5 = (bf16[144,512]{1,0:T(8,128)(2,1)S(1)}, bf16[144,512]{1,0:T(8,128)(2,1)S(1)}, u32[]{:S(2)}, u32[]{:S(2)}) collective-permute-start(bf16[144,512]{1,0:T(8,128)(2,1)S(1)} %get-tuple-element.11.refs_4_), channel_id=1, source_target_pairs={{0,12},{4,8},{8,4},{12,0},{1,13},{5,9},{9,5},{13,1},{2,14},{6,10},... | collective-permute-start | bytes 442376 | tf_op jit(solution)/shard_map/ppermute | solution.py:36
  5.8 0.5 %collective-permute-start.4 = (bf16[144,512]{1,0:T(8,128)(2,1)S(1)}, bf16[144,512]{1,0:T(8,128)(2,1)S(1)}, u32[]{:S(2)}, u32[]{:S(2)}) collective-permute-start(bf16[144,512]{1,0:T(8,128)(2,1)S(1)} %get-tuple-element.11.refs_4_), channel_id=1, source_target_pairs={{0,8},{4,12},{8,0},{12,4},{1,9},{5,13},{9,1},{13,5},{2,10},{6,14},... | collective-permute-start | bytes 442376 | tf_op jit(solution)/shard_map/ppermute | solution.py:36
  6.3 0.1 collective-permute-start.3
  6.5 4.0 %collective-permute-start.2 = (f32[136,128]{1,0:T(8,128)S(1)}, f32[136,128]{1,0:T(8,128)S(1)}, u32[]{:S(2)}, u32[]{:S(2)}) collective-permute-start(f32[136,128]{1,0:T(8,128)S(1)} %get-tuple-element.10), channel_id=1, source_target_pairs={{0,3},{1,2},{2,1},{3,0},{4,7},{5,6},{6,5},{7,4},{8,11},{9,10},{10,... | collective-permute-start | bytes 208904 | tf_op jit(solution)/shard_map/ppermute | solution.py:36
  10.5 0.0 collective-permute-start
  10.5 2.4 %collective-permute-done.2.refs_0_.refs_3_ = f32[136,128]{1,0:T(8,128)S(1)} collective-permute-done((f32[136,128]{1,0:T(8,128)S(1)}, f32[136,128]{1,0:T(8,128)S(1)}, u32[]{:S(2)}, u32[]{:S(2)}) %collective-permute-start.2) | collective-permute-done | bytes 69664 | tf_op jit(solution)/shard_map/ppermute | solution.py:36
  12.9 1.6 %collective-permute-start.1 = (f32[136,128]{1,0:T(8,128)S(1)}, f32[136,128]{1,0:T(8,128)S(1)}, u32[]{:S(2)}, u32[]{:S(2)}) collective-permute-start(f32[136,128]{1,0:T(8,128)S(1)} %get-tuple-element.9.refs_0_), channel_id=1, source_target_pairs={{0,2},{1,3},{2,0},{3,1},{4,6},{5,7},{6,4},{7,5},{8,10},{9,11},{10,... | collective-permute-start | bytes 208904 | tf_op jit(solution)/shard_map/ppermute | solution.py:36
  14.5 0.7 %slice.4.refs_8_ = s32[128,128]{1,0:T(8,128)S(1)} custom-call(f32[136,128]{1,0:T(8,128)S(1)} %get-tuple-element.9.refs_0_), custom_call_target="tpu_custom_call" | custom-call | tf_op jit(solution)/shard_map/slice/pallas_call | solution.py:387
  15.2 0.7 %slice.7.refs_11_ = s32[128,128]{1,0:T(8,128)S(1)} custom-call(f32[136,128]{1,0:T(8,128)S(1)} %collective-permute-done.2.refs_0_.refs_3_), custom_call_target="tpu_custom_call" | custom-call | tf_op jit(solution)/shard_map/slice/pallas_call | solution.py:387
  15.9 0.0 collective-permute-done.refs_0_.refs_1_
  15.9 0.7 %slice.5.refs_9_ = s32[128,128]{1,0:T(8,128)S(1)} custom-call(f32[136,128]{1,0:T(8,128)S(1)} %collective-permute-done.refs_0_.refs_1_), custom_call_target="tpu_custom_call" | custom-call | tf_op jit(solution)/shard_map/slice/pallas_call | solution.py:387
  16.7 0.0 copy-start
  16.7 1.4 %collective-permute-done.1.refs_0_.refs_2_ = f32[136,128]{1,0:T(8,128)S(1)} collective-permute-done((f32[136,128]{1,0:T(8,128)S(1)}, f32[136,128]{1,0:T(8,128)S(1)}, u32[]{:S(2)}, u32[]{:S(2)}) %collective-permute-start.1) | collective-permute-done | bytes 69664 | tf_op jit(solution)/shard_map/ppermute | solution.py:36
  18.1 0.7 %slice.6.refs_10_ = s32[128,128]{1,0:T(8,128)S(1)} custom-call(f32[136,128]{1,0:T(8,128)S(1)} %collective-permute-done.1.refs_0_.refs_2_), custom_call_target="tpu_custom_call" | custom-call | tf_op jit(solution)/shard_map/slice/pallas_call | solution.py:387
  18.8 0.0 collective-permute-done.5.refs_7_
  18.8 0.0 collective-permute-done.4.refs_6_
  18.8 0.0 collective-permute-done.3.refs_5_
  18.9 0.0 copy-done
  18.9 7.8 %frame.1.refs_0_ = f32[8,512]{1,0:T(8,128)S(1)} custom-call(f32[136,128]{1,0:T(8,128)S(1)} %get-tuple-element.9.refs_0_, f32[136,128]{1,0:T(8,128)S(1)} %collective-permute-done.refs_0_.refs_1_, f32[136,128]{1,0:T(8,128)S(1)} %collective-permute-done.1.refs_0_.refs_2_, f32[136,128]{1,0:T(8,128)S(1)} %collective-permute-done.2.refs_0_.refs_3_, ...), custom_call_target="tpu_custom_call" | custom-call | tf_op jit(solution)/shard_map/frame/pallas_call | solution.py:397
  26.7 0.1 collective-permute-start.8
  26.7 1.7 %collective-permute-start.7 = (f32[8,512]{1,0:T(8,128)S(1)}, f32[8,512]{1,0:T(8,128)S(1)}, u32[]{:S(2)}, u32[]{:S(2)}) collective-permute-start(f32[8,512]{1,0:T(8,128)S(1)} %frame.1.refs_0_), channel_id=1, source_target_pairs={{0,1},{1,0},{2,3},{3,2},{16,17},{17,16},{18,19},{19,18},{4,5},{5,4... | collective-permute-start | bytes 49160 | tf_op jit(solution)/shard_map/ppermute | solution.py:419
  28.4 0.2 collective-permute-start.6
  28.6 1.3 %collective-permute-done.8.refs_3_ = f32[8,512]{1,0:T(8,128)S(1)} collective-permute-done((f32[8,512]{1,0:T(8,128)S(1)}, f32[8,512]{1,0:T(8,128)S(1)}, u32[]{:S(2)}, u32[]{:S(2)}) %collective-permute-start.8) | collective-permute-done | bytes 16416 | tf_op jit(solution)/shard_map/ppermute | solution.py:419
  29.9 0.7 %collective-permute-done.7.refs_2_ = f32[8,512]{1,0:T(8,128)S(1)} collective-permute-done((f32[8,512]{1,0:T(8,128)S(1)}, f32[8,512]{1,0:T(8,128)S(1)}, u32[]{:S(2)}, u32[]{:S(2)}) %collective-permute-start.7) | collective-permute-done | bytes 16416 | tf_op jit(solution)/shard_map/ppermute | solution.py:419
  30.5 0.0 collective-permute-done.6.refs_1_
  30.6 0.7 %emit.1 = (f32[2,128]{1,0:T(2,128)}, f32[2]{0:T(128)}, f32[3,2,128]{2,1,0:T(2,128)}) custom-call(f32[8,512]{1,0:T(8,128)S(1)} %frame.1.refs_0_, f32[8,512]{1,0:T(8,128)S(1)} %collective-permute-done.6.refs_1_, f32[8,512]{1,0:T(8,128)S(1)} %collective-permute-done.7.refs_2_, f32[8,512]{1,0:T(8,128)S(1)} %collective-permute-done.8.refs_3_), custom_call_target="tpu_custom_call" | custom-call | tf_op jit(solution)/shard_map/emit/pallas_call | solution.py:422
Async XLA Ops:
  1.9 17.0 %collective-permute-start.5 = (bf16[144,512]{1,0:T(8,128)(2,1)S(1)}, bf16[144,512]{1,0:T(8,128)(2,1)S(1)}, u32[]{:S(2)}, u32[]{:S(2)}) collective-permute-start(bf16[144,512]{1,0:T(8,128)(2,1)S(1)} %get-tuple-element.11.refs_4_), channel_id=1, source_target_pairs={{0,12},{4,8},{8,4},{12,0},{1,13},{5,9},{9,5},{13,1},{2,14},{6,10},... | collective-permute-start | bytes 442376 | tf_op jit(solution)/shard_map/ppermute | solution.py:36
  5.8 13.0 %collective-permute-start.4 = (bf16[144,512]{1,0:T(8,128)(2,1)S(1)}, bf16[144,512]{1,0:T(8,128)(2,1)S(1)}, u32[]{:S(2)}, u32[]{:S(2)}) collective-permute-start(bf16[144,512]{1,0:T(8,128)(2,1)S(1)} %get-tuple-element.11.refs_4_), channel_id=1, source_target_pairs={{0,8},{4,12},{8,0},{12,4},{1,9},{5,13},{9,1},{13,5},{2,10},{6,14},... | collective-permute-start | bytes 442376 | tf_op jit(solution)/shard_map/ppermute | solution.py:36
  6.3 12.5 %collective-permute-start.3 = (bf16[144,512]{1,0:T(8,128)(2,1)S(1)}, bf16[144,512]{1,0:T(8,128)(2,1)S(1)}, u32[]{:S(2)}, u32[]{:S(2)}) collective-permute-start(bf16[144,512]{1,0:T(8,128)(2,1)S(1)} %get-tuple-element.11.refs_4_), channel_id=1, source_target_pairs={{0,4},{4,0},{8,12},{12,8},{1,5},{5,1},{9,13},{13,9},{2,6},{6,2},{1... | collective-permute-start | bytes 442376 | tf_op jit(solution)/shard_map/ppermute | solution.py:36
  6.5 6.4 %collective-permute-start.2 = (f32[136,128]{1,0:T(8,128)S(1)}, f32[136,128]{1,0:T(8,128)S(1)}, u32[]{:S(2)}, u32[]{:S(2)}) collective-permute-start(f32[136,128]{1,0:T(8,128)S(1)} %get-tuple-element.10), channel_id=1, source_target_pairs={{0,3},{1,2},{2,1},{3,0},{4,7},{5,6},{6,5},{7,4},{8,11},{9,10},{10,... | collective-permute-start | bytes 208904 | tf_op jit(solution)/shard_map/ppermute | solution.py:36
  10.5 5.5 %collective-permute-start = (f32[136,128]{1,0:T(8,128)S(1)}, f32[136,128]{1,0:T(8,128)S(1)}, u32[]{:S(2)}, u32[]{:S(2)}) collective-permute-start(f32[136,128]{1,0:T(8,128)S(1)} %get-tuple-element.10), channel_id=1, source_target_pairs={{0,1},{1,0},{2,3},{3,2},{4,5},{5,4},{6,7},{7,6},{8,9},{9,8},{10,11... | collective-permute-start | bytes 208904 | tf_op jit(solution)/shard_map/ppermute | solution.py:36
  12.9 5.2 %collective-permute-start.1 = (f32[136,128]{1,0:T(8,128)S(1)}, f32[136,128]{1,0:T(8,128)S(1)}, u32[]{:S(2)}, u32[]{:S(2)}) collective-permute-start(f32[136,128]{1,0:T(8,128)S(1)} %get-tuple-element.9.refs_0_), channel_id=1, source_target_pairs={{0,2},{1,3},{2,0},{3,1},{4,6},{5,7},{6,4},{7,5},{8,10},{9,11},{10,... | collective-permute-start | bytes 208904 | tf_op jit(solution)/shard_map/ppermute | solution.py:36
  16.7 2.2 %copy-start = (bf16[1,128,128]{2,1,0:T(8,128)(2,1)S(1)}, bf16[1,128,128]{2,1,0:T(8,128)(2,1)}, u32[]{:S(2)}) copy-start(bf16[1,128,128]{2,1,0:T(8,128)(2,1)} %param.13) | copy-start | bytes 98308
  26.7 3.2 %collective-permute-start.8 = (f32[8,512]{1,0:T(8,128)S(1)}, f32[8,512]{1,0:T(8,128)S(1)}, u32[]{:S(2)}, u32[]{:S(2)}) collective-permute-start(f32[8,512]{1,0:T(8,128)S(1)} %frame.1.refs_0_), channel_id=1, source_target_pairs={{0,17},{1,16},{2,19},{3,18},{16,1},{17,0},{18,3},{19,2},{4,21},{5,... | collective-permute-start | bytes 49160 | tf_op jit(solution)/shard_map/ppermute | solution.py:419
  26.7 3.8 %collective-permute-start.7 = (f32[8,512]{1,0:T(8,128)S(1)}, f32[8,512]{1,0:T(8,128)S(1)}, u32[]{:S(2)}, u32[]{:S(2)}) collective-permute-start(f32[8,512]{1,0:T(8,128)S(1)} %frame.1.refs_0_), channel_id=1, source_target_pairs={{0,1},{1,0},{2,3},{3,2},{16,17},{17,16},{18,19},{19,18},{4,5},{5,4... | collective-permute-start | bytes 49160 | tf_op jit(solution)/shard_map/ppermute | solution.py:419
  28.4 2.1 %collective-permute-start.6 = (f32[8,512]{1,0:T(8,128)S(1)}, f32[8,512]{1,0:T(8,128)S(1)}, u32[]{:S(2)}, u32[]{:S(2)}) collective-permute-start(f32[8,512]{1,0:T(8,128)S(1)} %frame.1.refs_0_), channel_id=1, source_target_pairs={{0,16},{1,17},{2,18},{3,19},{16,0},{17,1},{18,2},{19,3},{4,20},{5,... | collective-permute-start | bytes 49160 | tf_op jit(solution)/shard_map/ppermute | solution.py:419
where the time goes:
time: 31.5 us; the launch traced here: 31.2 us
  Pallas kernels  12.6 us (40%)
  starting transfers between devices  12.1 us (38%)
  waiting for transfers between devices  5.76 us (18%)
  between operations  0.73 us (2%)
    ppermute x6, starting transfers between devices, exchange(): lax.ppermute(x, axis, [(i, dest(axis_size, i, r)) for i in range(axis_siz...  10.2 us
    pallas_call x1, Pallas kernels, body(): pl.pallas_call(lambda *refs: frame_kernel(n_section, n_atoms, heads, slot...  7.79 us
    ppermute x6, waiting for transfers between devices, exchange(): lax.ppermute(x, axis, [(i, dest(axis_size, i, r)) for i in range(axis_siz...  3.8 us
    pallas_call x4, Pallas kernels, body(): pl.pallas_call(lambda *refs: slice_kernel(total, *refs), out_shape=shape(...  2.92 us
    ppermute x3, waiting for transfers between devices, joint(): return lax.ppermute(force, ('member', 'atoms'), pairs)  1.96 us
    ppermute x3, starting transfers between devices, joint(): return lax.ppermute(force, ('member', 'atoms'), pairs)  1.92 us
    pallas_call x1, Pallas kernels, body(): pl.pallas_call(lambda *refs: pack_kernel(n_section, *refs), out_shape=[sh...  1.21 us
    pallas_call x1, Pallas kernels, body(): pl.pallas_call(lambda *refs: emit_kernel(n_member, n_atoms, count, *refs)...  0.68 us
  transfers between devices with their start and end apart: 9, of which 4 were waited for; matrix products, arithmetic and copies ran while one was open for 0% of the time, Pallas kernels for 9%

commit v1 on v0

--- a/solution.py
+++ b/solution.py
@@ -15,6 +15,7 @@
 LAG = 2
 WROWS = 16
 FRAME_PARAMS = pltpu.CompilerParams(vmem_limit_bytes=32 << 20)
+PAIRS_PARAMS = pltpu.CompilerParams(vmem_limit_bytes=16 << 20)
 SMALL_PARAMS = pltpu.CompilerParams(vmem_limit_bytes=8 << 20)
 
 
@@ -119,16 +120,45 @@
     count_slots(msg_ref, msg_ref.shape[0] - EXTRA, total, cnt_ref)
 
 
+def pairs_kernel(n_atoms, *refs):
+    msgs, cnt_v = refs[:n_atoms], refs[n_atoms : 2 * n_atoms]
+    table_ref, p_ref, h_ref, ext_v = refs[2 * n_atoms :]
+    slots = msgs[0].shape[0] - EXTRA
+    count = msgs[0].shape[1]
+    total = n_atoms * count
+    low = total // NIBBLES
+    a_idx = lax.axis_index("atoms")
+    ext = [msgs[r][slots:, :] for r in range(n_atoms)]
+    types = jnp.concatenate(ext, axis=1)[3:4].astype(jnp.int32)
+    iota_t = lax.broadcasted_iota(jnp.int32, (table_ref.shape[0], total), 0)
+    onehot = (iota_t == types).astype(BF16)
+    h_ref[...] = dot(jnp.transpose(table_ref[...]), onehot)
+    for r in range(n_atoms):
+        ext_v[source(n_atoms, a_idx, r)] = ext[r]
+    pos_col = jnp.concatenate([jnp.transpose(ext_v[b]) for b in range(n_atoms)], axis=0)
+    for n in range(NIBBLES):
+        part = pos_col[n * low : (n + 1) * low]
+        cols = [jnp.broadcast_to(part[:, c : c + 1], (low, count)) for c in range(3)]
+        for r in range(n_atoms):
+            acc = cnt_v[r][low:, :] if n % 2 else cnt_v[r][:low, :]
+            hits = (lax.shift_right_logical(acc, 8 * (n // 2)) & 0xFF).astype(F32)
+            dist = None
+            for c in range(3):
+                delta = cols[c] - ext[r][c : c + 1, :]
+                dist = delta * delta if dist is None else dist + delta * delta
+            p_ref[n * low : (n + 1) * low, r * count : (r + 1) * count] = hits / (
+                2.0 + 0.25 * dist
+            )
+
+
 def frame_kernel(n_section, n_atoms, heads, slots, *refs):
     msgs, refs = refs[:n_atoms], refs[n_atoms:]
     weights_in, refs = refs[:n_section], refs[n_section:]
-    cnt_v, refs = refs[:n_atoms], refs[n_atoms:]
-    table_ref, out_ref, ext_v, w_v, p_v = refs
+    p_v, embed_ref, out_ref, w_v = refs
     count = msgs[0].shape[1]
     total = n_atoms * count
-    width = table_ref.shape[1]
+    width = embed_ref.shape[0]
     head_dim = width // heads
-    low = total // NIBBLES
     a_idx = lax.axis_index("atoms")
     s_idx = lax.axis_index("section")
     tile = max(count, min(256, total // 4))
@@ -136,45 +166,25 @@
     per_tile = tile // count
     group = max(1, 256 // tile)
     span = [slice(t * tile, (t + 1) * tile) for t in range(tiles)]
-
     for r in range(n_section):
-        w = weights_in[r][...]
-        side = w.shape[0] - WROWS
-        gain = jnp.transpose(
-            jnp.broadcast_to(w[side : side + 1, :side].astype(F32), (side, side))
-        ).astype(BF16)
-        w_v[source(n_section, s_idx, r)] = jnp.concatenate(
-            [jnp.transpose(w[:side]), gain, w[side:, :side], w[side:, side : 2 * side]], axis=0
-        )
-
-    ext = [msgs[r][slots:, :] for r in range(n_atoms)]
-    for r in range(n_atoms):
-        ext_v[source(n_atoms, a_idx, r)] = ext[r]
-    pos_col = jnp.concatenate([jnp.transpose(ext_v[b]) for b in range(n_atoms)], axis=0)
-    pos = jnp.concatenate(ext, axis=1)[:3]
+        w_v[source(n_section, s_idx, r)] = weights_in[r][...]
+    pos = jnp.concatenate([msgs[r][slots:, :] for r in range(n_atoms)], axis=1)[:3]
     pos_hi = pos.astype(BF16).astype(F32)
     tail = jnp.concatenate(
         [pos_hi, pos - pos_hi, jnp.ones((1, total), F32), jnp.zeros((9, total), F32)], axis=0
     ).astype(BF16)
-    types = jnp.concatenate(ext, axis=1)[3:4].astype(jnp.int32)
-    iota_t = lax.broadcasted_iota(jnp.int32, (table_ref.shape[0], total), 0)
-    onehot = (iota_t == types).astype(BF16)
-    embed = dot(jnp.transpose(table_ref[...]), onehot)
-
-    def pairs(r):
-        lanes = slice(r * count, (r + 1) * count)
-        for n in range(NIBBLES):
-            acc = cnt_v[r][low:, :] if n % 2 else cnt_v[r][:low, :]
-            hits = (lax.shift_right_logical(acc, 8 * (n // 2)) & 0xFF).astype(F32)
-            part = pos_col[n * low : (n + 1) * low]
-            dist = None
-            for c in range(3):
-                delta = part[:, c : c + 1] - ext[r][c : c + 1, :]
-                dist = delta * delta if dist is None else dist + delta * delta
-            p_v[n * low : (n + 1) * low, lanes] = 0.5 * hits / (1.0 + 0.125 * dist)
 
     scale = 0.5 / math.sqrt(head_dim)
-    h = [embed[:, span[t]] for t in range(tiles)]
+    h = [embed_ref[:, span[t]] for t in range(tiles)]
+    params = {}
+
+    def load(b):
+        w = w_v[b]
+        row = w[width:]
+        gain = jnp.transpose(jnp.broadcast_to(row[:1, :width].astype(F32), (width, width)))
+        coef = row[:1, width : width + heads].astype(F32)
+        params[b] = jnp.transpose(w[:width]), gain, coef
+
     state = {}
     force = [None] * tiles
     results = {}
@@ -186,10 +196,12 @@
         return zeros[n]
 
     def project(b, t):
-        w = w_v[b]
+        if b not in params:
+            load(b)
+        w, gain, _ = params[b]
         norm = lax.rsqrt(jnp.mean(h[t] * h[t], axis=0, keepdims=True) + 1e-06)
-        x = (h[t] * norm * w[4 * width : 5 * width, :1].astype(F32)).astype(BF16)
-        qkv = dot(w[: 3 * width, :width], x)
+        x = (h[t] * norm * gain[:, :1]).astype(BF16)
+        qkv = dot(w[: 3 * width], x)
         k = jnp.transpose(qkv[width : 2 * width].astype(BF16))
         q = (qkv[:width] * scale).astype(BF16)
         v = qkv[2 * width :].astype(BF16)
@@ -240,14 +252,13 @@
             results[key] = own
 
     def finish(b, t):
-        w = w_v[b]
+        w, _, coef = params[b]
         parts = [results.pop((b, t, hd)) for hd in range(heads)]
         if b + 1 < n_section:
             msg = jnp.concatenate([part[0] for part in parts], axis=0) * (1.0 / slots)
-            step = dot(w[3 * width : 4 * width], msg.astype(BF16))
+            step = dot(w[3 * width :], msg.astype(BF16))
             h[t] = (h[t] + step).astype(BF16).astype(F32)
             project(b + 1, t)
-        coef = w[5 * width + WROWS : 5 * width + WROWS + 1, :heads].astype(F32)
         for hd, part in enumerate(parts):
             term = coef[:, hd : hd + 1] * part[1]
             force[t] = term if force[t] is None else force[t] + term
@@ -260,7 +271,6 @@
         (b, t, jt, g) for b in range(n_section) for t, jt in order for g in range(heads // group)
     ]
     left = {(b, t): tiles * (heads // group) for b in range(n_section) for t in range(tiles)}
-    ready = set()
     pending, gated = [], []
 
     def retire():
@@ -279,11 +289,6 @@
 
     def gate():
         unit, value = pending.pop(0)
-        _, t = unit[:2]
-        for r in range(t * per_tile, (t + 1) * per_tile):
-            if r not in ready:
-                ready.add(r)
-                pairs(r)
         gated.append((unit, consume(unit, value)))
 
     for t in range(tiles):
@@ -394,19 +399,24 @@
             )(msg)
             for msg in lists
         ]
+        pair, embed = pl.pallas_call(
+            lambda *refs: pairs_kernel(n_atoms, *refs),
+            out_shape=[shape((total, total), F32), shape((width, total), F32)],
+            in_specs=[vmem] * (2 * n_atoms + 1),
+            out_specs=[vmem, vmem],
+            scratch_shapes=[pltpu.VMEM((n_atoms, EXTRA, count), F32)],
+            compiler_params=PAIRS_PARAMS,
+            name="pairs",
+        )(*lists, *counted, type_table[0])
         force = pl.pallas_call(
             lambda *refs: frame_kernel(n_section, n_atoms, heads, slots, *refs),
             out_shape=shape((8, total), F32),
-            in_specs=[vmem] * (2 * n_atoms + n_section + 1),
+            in_specs=[vmem] * (n_atoms + n_section + 2),
             out_specs=vmem,
-            scratch_shapes=[
-                pltpu.VMEM((n_atoms, EXTRA, count), F32),
-                pltpu.VMEM((n_section, 5 * width + 2 * WROWS, width), BF16),
-                pltpu.VMEM((total, total), F32),
-            ],
+            scratch_shapes=[pltpu.VMEM((n_section, width + WROWS, 4 * width), BF16)],
             compiler_params=FRAME_PARAMS,
             name="frame",
-        )(*lists, *weights, *counted, type_table[0])
+        )(*lists, *weights, pair, embed)
 
         def joint(x, r):
             if x == 0 and r == 0:

time: 31.5 us -> 32.4 us (1.029)
  starting transfers between devices: 12.1 us -> 15.8 us
  waiting for transfers between devices: 5.76 us -> 2.96 us
    ppermute x6, starting transfers between devices: 10.2 us -> 13.9 us  [exchange(): lax.ppermute(x, axis, [(i, dest(axis_size, i, r)) for i in range(axis_siz...]
    ppermute x6, waiting for transfers between devices: 3.8 us -> 1 us  [exchange(): lax.ppermute(x, axis, [(i, dest(axis_size, i, r)) for i in range(axis_siz...]
    pallas_call x1, Pallas kernels: 7.79 us -> 6.98 us  [body(): pl.pallas_call(lambda *refs: frame_kernel(n_section, n_atoms, heads, slot...]
    pallas_call x0 -> x1, Pallas kernels: none -> 0.77 us  [body(): pl.pallas_call(lambda *refs: pairs_kernel(n_atoms, *refs), out_shape=[sha...]
  transfers between devices with their start and end apart: 9 -> 9, of which waited for: 4 -> 3; matrix products, arithmetic and copies ran while one was open for 0% -> 0% of each run, Pallas kernels for 9% -> 11%
where the time goes in v1:
time: 32.4 us; the launch traced here: 32.1 us
  starting transfers between devices  15.8 us (49%)
  Pallas kernels  12.6 us (39%)
  waiting for transfers between devices  2.96 us (9%)
  between operations  0.74 us (2%)
    ppermute x6, starting transfers between devices, exchange(): lax.ppermute(x, axis, [(i, dest(axis_size, i, r)) for i in range(axis_siz...  13.9 us
    pallas_call x1, Pallas kernels, body(): pl.pallas_call(lambda *refs: frame_kernel(n_section, n_atoms, heads, slot...  6.98 us
    pallas_call x4, Pallas kernels, body(): pl.pallas_call(lambda *refs: slice_kernel(total, *refs), out_shape=shape(...  2.92 us
    ppermute x3, waiting for transfers between devices, joint(): return lax.ppermute(force, ('member', 'atoms'), pairs)  1.96 us
    ppermute x3, starting transfers between devices, joint(): return lax.ppermute(force, ('member', 'atoms'), pairs)  1.91 us
    pallas_call x1, Pallas kernels, body(): pl.pallas_call(lambda *refs: pack_kernel(n_section, *refs), out_shape=[sh...  1.21 us
    ppermute x6, waiting for transfers between devices, exchange(): lax.ppermute(x, axis, [(i, dest(axis_size, i, r)) for i in range(axis_siz...  1 us
    pallas_call x1, Pallas kernels, body(): pl.pallas_call(lambda *refs: pairs_kernel(n_atoms, *refs), out_shape=[sha...  0.77 us
  transfers between devices with their start and end apart: 9, of which 3 were waited for; matrix products, arithmetic and copies ran while one was open for 0% of the time, Pallas kernels for 11%

profile of v1, /device:TPU:0, one launch (start us, length us, event | category | flops | bytes accessed | tf_op | source)
XLA Modules:
  0.0 32.1 jit_solution(17256358905289093056)
XLA Ops:
  0.6 1.2 %pack.1 = (f32[136,128]{1,0:T(8,128)S(1)}, f32[136,128]{1,0:T(8,128)S(1)}, bf16[144,512]{1,0:T(8,128)(2,1)S(1)}) custom-call(f32[3,8,128]{2,1,0:T(8,128)} %bitcast.10, s32[8,128]{1,0:T(8,128)} %refs_1_.1, s32[8,128,128]{2,1,0:T(8,128)} %refs_2_.1, s32[8,128,128]{2,1,0:T(8,128)} %refs_3_.1, bf16[128,384]{1,0:T(8,128)(2,1)} %bitcast.8, ...), custom_call_target="tpu_custom_call" | custom-call | tf_op jit(solution)/shard_map/pack/pallas_call | solution.py:355
  1.9 3.0 %collective-permute-start.3 = (bf16[144,512]{1,0:T(8,128)(2,1)S(1)}, bf16[144,512]{1,0:T(8,128)(2,1)S(1)}, u32[]{:S(2)}, u32[]{:S(2)}) collective-permute-start(bf16[144,512]{1,0:T(8,128)(2,1)S(1)} %get-tuple-element.13.refs_4_), channel_id=1, source_target_pairs={{0,4},{4,0},{8,12},{12,8},{1,5},{5,1},{9,13},{13,9},{2,6},{6,2},{1... | collective-permute-start | bytes 442376 | tf_op jit(solution)/shard_map/ppermute | solution.py:37
  4.9 1.5 %collective-permute-start.4 = (bf16[144,512]{1,0:T(8,128)(2,1)S(1)}, bf16[144,512]{1,0:T(8,128)(2,1)S(1)}, u32[]{:S(2)}, u32[]{:S(2)}) collective-permute-start(bf16[144,512]{1,0:T(8,128)(2,1)S(1)} %get-tuple-element.13.refs_4_), channel_id=1, source_target_pairs={{0,8},{4,12},{8,0},{12,4},{1,9},{5,13},{9,1},{13,5},{2,10},{6,14},... | collective-permute-start | bytes 442376 | tf_op jit(solution)/shard_map/ppermute | solution.py:37
  6.4 0.0 collective-permute-start.5
  6.4 3.0 %collective-permute-start.1 = (f32[136,128]{1,0:T(8,128)S(1)}, f32[136,128]{1,0:T(8,128)S(1)}, u32[]{:S(2)}, u32[]{:S(2)}) collective-permute-start(f32[136,128]{1,0:T(8,128)S(1)} %get-tuple-element.11.refs_0_), channel_id=1, source_target_pairs={{0,2},{1,3},{2,0},{3,1},{4,6},{5,7},{6,4},{7,5},{8,10},{9,11},{10,... | collective-permute-start | bytes 208904 | tf_op jit(solution)/shard_map/ppermute | solution.py:37
  9.5 1.6 %collective-permute-start = (f32[136,128]{1,0:T(8,128)S(1)}, f32[136,128]{1,0:T(8,128)S(1)}, u32[]{:S(2)}, u32[]{:S(2)}) collective-permute-start(f32[136,128]{1,0:T(8,128)S(1)} %get-tuple-element.12), channel_id=1, source_target_pairs={{0,1},{1,0},{2,3},{3,2},{4,5},{5,4},{6,7},{7,6},{8,9},{9,8},{10,11... | collective-permute-start | bytes 208904 | tf_op jit(solution)/shard_map/ppermute | solution.py:37
  11.1 0.9 %collective-permute-done.1.refs_0_.refs_2_ = f32[136,128]{1,0:T(8,128)S(1)} collective-permute-done((f32[136,128]{1,0:T(8,128)S(1)}, f32[136,128]{1,0:T(8,128)S(1)}, u32[]{:S(2)}, u32[]{:S(2)}) %collective-permute-start.1) | collective-permute-done | bytes 69664 | tf_op jit(solution)/shard_map/ppermute | solution.py:37
  12.0 4.7 %collective-permute-start.2 = (f32[136,128]{1,0:T(8,128)S(1)}, f32[136,128]{1,0:T(8,128)S(1)}, u32[]{:S(2)}, u32[]{:S(2)}) collective-permute-start(f32[136,128]{1,0:T(8,128)S(1)} %get-tuple-element.12), channel_id=1, source_target_pairs={{0,3},{1,2},{2,1},{3,0},{4,7},{5,6},{6,5},{7,4},{8,11},{9,10},{10,... | collective-permute-start | bytes 208904 | tf_op jit(solution)/shard_map/ppermute | solution.py:37
  16.7 0.7 %slice.4.refs_4_ = s32[128,128]{1,0:T(8,128)S(1)} custom-call(f32[136,128]{1,0:T(8,128)S(1)} %get-tuple-element.11.refs_0_), custom_call_target="tpu_custom_call" | custom-call | tf_op jit(solution)/shard_map/slice/pallas_call | solution.py:392
  17.4 0.7 %slice.6.refs_6_ = s32[128,128]{1,0:T(8,128)S(1)} custom-call(f32[136,128]{1,0:T(8,128)S(1)} %collective-permute-done.1.refs_0_.refs_2_), custom_call_target="tpu_custom_call" | custom-call | tf_op jit(solution)/shard_map/slice/pallas_call | solution.py:392
  18.1 0.0 collective-permute-done.refs_0_.refs_1_
  18.2 0.7 %slice.5.refs_5_ = s32[128,128]{1,0:T(8,128)S(1)} custom-call(f32[136,128]{1,0:T(8,128)S(1)} %collective-permute-done.refs_0_.refs_1_), custom_call_target="tpu_custom_call" | custom-call | tf_op jit(solution)/shard_map/slice/pallas_call | solution.py:392
  18.9 0.0 copy-start
  18.9 0.1 collective-permute-done.2.refs_0_.refs_3_
  19.0 0.7 %slice.7.refs_7_ = s32[128,128]{1,0:T(8,128)S(1)} custom-call(f32[136,128]{1,0:T(8,128)S(1)} %collective-permute-done.2.refs_0_.refs_3_), custom_call_target="tpu_custom_call" | custom-call | tf_op jit(solution)/shard_map/slice/pallas_call | solution.py:392
  19.7 0.0 copy-done
  19.7 0.8 %pairs.1 = (f32[512,512]{1,0:T(8,128)S(1)}, f32[128,512]{1,0:T(8,128)S(1)}) custom-call(f32[136,128]{1,0:T(8,128)S(1)} %get-tuple-element.11.refs_0_, f32[136,128]{1,0:T(8,128)S(1)} %collective-permute-done.refs_0_.refs_1_, f32[136,128]{1,0:T(8,128)S(1)} %collective-permute-done.1.refs_0_.refs_2_, f32[136,128]{1,0:T(8,128)S(1)} %collective-permute-done.2.refs_0_.refs_3_, ...), custom_call_target="tpu_custom_call" | custom-call | tf_op jit(solution)/shard_map/pairs/pallas_call | solution.py:402
  20.5 0.0 collective-permute-done.3.refs_5_
  20.5 0.0 collective-permute-done.4.refs_6_
  20.5 0.0 collective-permute-done.5.refs_7_
  20.5 7.0 %frame.1.refs_0_ = f32[8,512]{1,0:T(8,128)S(1)} custom-call(f32[136,128]{1,0:T(8,128)S(1)} %get-tuple-element.11.refs_0_, f32[136,128]{1,0:T(8,128)S(1)} %collective-permute-done.refs_0_.refs_1_, f32[136,128]{1,0:T(8,128)S(1)} %collective-permute-done.1.refs_0_.refs_2_, f32[136,128]{1,0:T(8,128)S(1)} %collective-permute-done.2.refs_0_.refs_3_, ...), custom_call_target="tpu_custom_call" | custom-call | tf_op jit(solution)/shard_map/frame/pallas_call | solution.py:411
  27.5 0.1 collective-permute-start.6
  27.6 0.1 collective-permute-start.7
  27.7 1.8 %collective-permute-start.8 = (f32[8,512]{1,0:T(8,128)S(1)}, f32[8,512]{1,0:T(8,128)S(1)}, u32[]{:S(2)}, u32[]{:S(2)}) collective-permute-start(f32[8,512]{1,0:T(8,128)S(1)} %frame.1.refs_0_), channel_id=1, source_target_pairs={{0,17},{1,16},{2,19},{3,18},{16,1},{17,0},{18,3},{19,2},{4,21},{5,... | collective-permute-start | bytes 49160 | tf_op jit(solution)/shard_map/ppermute | solution.py:429
  29.4 0.0 collective-permute-done.6.refs_1_
  29.4 2.0 %collective-permute-done.7.refs_2_ = f32[8,512]{1,0:T(8,128)S(1)} collective-permute-done((f32[8,512]{1,0:T(8,128)S(1)}, f32[8,512]{1,0:T(8,128)S(1)}, u32[]{:S(2)}, u32[]{:S(2)}) %collective-permute-start.7) | collective-permute-done | bytes 16416 | tf_op jit(solution)/shard_map/ppermute | solution.py:429
  31.4 0.0 collective-permute-done.8.refs_3_
  31.4 0.7 %emit.1 = (f32[2,128]{1,0:T(2,128)}, f32[2]{0:T(128)}, f32[3,2,128]{2,1,0:T(2,128)}) custom-call(f32[8,512]{1,0:T(8,128)S(1)} %frame.1.refs_0_, f32[8,512]{1,0:T(8,128)S(1)} %collective-permute-done.6.refs_1_, f32[8,512]{1,0:T(8,128)S(1)} %collective-permute-done.7.refs_2_, f32[8,512]{1,0:T(8,128)S(1)} %collective-permute-done.8.refs_3_), custom_call_target="tpu_custom_call" | custom-call | tf_op jit(solution)/shard_map/emit/pallas_call | solution.py:432
Async XLA Ops:
  1.9 18.6 %collective-permute-start.3 = (bf16[144,512]{1,0:T(8,128)(2,1)S(1)}, bf16[144,512]{1,0:T(8,128)(2,1)S(1)}, u32[]{:S(2)}, u32[]{:S(2)}) collective-permute-start(bf16[144,512]{1,0:T(8,128)(2,1)S(1)} %get-tuple-element.13.refs_4_), channel_id=1, source_target_pairs={{0,4},{4,0},{8,12},{12,8},{1,5},{5,1},{9,13},{13,9},{2,6},{6,2},{1... | collective-permute-start | bytes 442376 | tf_op jit(solution)/shard_map/ppermute | solution.py:37
  4.9 15.6 %collective-permute-start.4 = (bf16[144,512]{1,0:T(8,128)(2,1)S(1)}, bf16[144,512]{1,0:T(8,128)(2,1)S(1)}, u32[]{:S(2)}, u32[]{:S(2)}) collective-permute-start(bf16[144,512]{1,0:T(8,128)(2,1)S(1)} %get-tuple-element.13.refs_4_), channel_id=1, source_target_pairs={{0,8},{4,12},{8,0},{12,4},{1,9},{5,13},{9,1},{13,5},{2,10},{6,14},... | collective-permute-start | bytes 442376 | tf_op jit(solution)/shard_map/ppermute | solution.py:37
  6.4 14.1 %collective-permute-start.5 = (bf16[144,512]{1,0:T(8,128)(2,1)S(1)}, bf16[144,512]{1,0:T(8,128)(2,1)S(1)}, u32[]{:S(2)}, u32[]{:S(2)}) collective-permute-start(bf16[144,512]{1,0:T(8,128)(2,1)S(1)} %get-tuple-element.13.refs_4_), channel_id=1, source_target_pairs={{0,12},{4,8},{8,4},{12,0},{1,13},{5,9},{9,5},{13,1},{2,14},{6,10},... | collective-permute-start | bytes 442376 | tf_op jit(solution)/shard_map/ppermute | solution.py:37
  6.4 5.5 %collective-permute-start.1 = (f32[136,128]{1,0:T(8,128)S(1)}, f32[136,128]{1,0:T(8,128)S(1)}, u32[]{:S(2)}, u32[]{:S(2)}) collective-permute-start(f32[136,128]{1,0:T(8,128)S(1)} %get-tuple-element.11.refs_0_), channel_id=1, source_target_pairs={{0,2},{1,3},{2,0},{3,1},{4,6},{5,7},{6,4},{7,5},{8,10},{9,11},{10,... | collective-permute-start | bytes 208904 | tf_op jit(solution)/shard_map/ppermute | solution.py:37
  9.5 8.7 %collective-permute-start = (f32[136,128]{1,0:T(8,128)S(1)}, f32[136,128]{1,0:T(8,128)S(1)}, u32[]{:S(2)}, u32[]{:S(2)}) collective-permute-start(f32[136,128]{1,0:T(8,128)S(1)} %get-tuple-element.12), channel_id=1, source_target_pairs={{0,1},{1,0},{2,3},{3,2},{4,5},{5,4},{6,7},{7,6},{8,9},{9,8},{10,11... | collective-permute-start | bytes 208904 | tf_op jit(solution)/shard_map/ppermute | solution.py:37
  12.0 7.0 %collective-permute-start.2 = (f32[136,128]{1,0:T(8,128)S(1)}, f32[136,128]{1,0:T(8,128)S(1)}, u32[]{:S(2)}, u32[]{:S(2)}) collective-permute-start(f32[136,128]{1,0:T(8,128)S(1)} %get-tuple-element.12), channel_id=1, source_target_pairs={{0,3},{1,2},{2,1},{3,0},{4,7},{5,6},{6,5},{7,4},{8,11},{9,10},{10,... | collective-permute-start | bytes 208904 | tf_op jit(solution)/shard_map/ppermute | solution.py:37
  18.9 0.8 %copy-start = (bf16[1,128,128]{2,1,0:T(8,128)(2,1)S(1)}, bf16[1,128,128]{2,1,0:T(8,128)(2,1)}, u32[]{:S(2)}) copy-start(bf16[1,128,128]{2,1,0:T(8,128)(2,1)} %param.13) | copy-start | bytes 98308
  27.5 1.9 %collective-permute-start.6 = (f32[8,512]{1,0:T(8,128)S(1)}, f32[8,512]{1,0:T(8,128)S(1)}, u32[]{:S(2)}, u32[]{:S(2)}) collective-permute-start(f32[8,512]{1,0:T(8,128)S(1)} %frame.1.refs_0_), channel_id=1, source_target_pairs={{0,16},{1,17},{2,18},{3,19},{16,0},{17,1},{18,2},{19,3},{4,20},{5,... | collective-permute-start | bytes 49160 | tf_op jit(solution)/shard_map/ppermute | solution.py:429
  27.6 3.8 %collective-permute-start.7 = (f32[8,512]{1,0:T(8,128)S(1)}, f32[8,512]{1,0:T(8,128)S(1)}, u32[]{:S(2)}, u32[]{:S(2)}) collective-permute-start(f32[8,512]{1,0:T(8,128)S(1)} %frame.1.refs_0_), channel_id=1, source_target_pairs={{0,1},{1,0},{2,3},{3,2},{16,17},{17,16},{18,19},{19,18},{4,5},{5,4... | collective-permute-start | bytes 49160 | tf_op jit(solution)/shard_map/ppermute | solution.py:429
  27.7 3.7 %collective-permute-start.8 = (f32[8,512]{1,0:T(8,128)S(1)}, f32[8,512]{1,0:T(8,128)S(1)}, u32[]{:S(2)}, u32[]{:S(2)}) collective-permute-start(f32[8,512]{1,0:T(8,128)S(1)} %frame.1.refs_0_), channel_id=1, source_target_pairs={{0,17},{1,16},{2,19},{3,18},{16,1},{17,0},{18,3},{19,2},{4,21},{5,... | collective-permute-start | bytes 49160 | tf_op jit(solution)/shard_map/ppermute | solution.py:429

commit v2 on v1

--- a/solution.py
+++ b/solution.py
@@ -11,7 +11,7 @@
 BF16 = jnp.bfloat16
 EXTRA = 8
 NIBBLES = 8
-AHEAD = 6
+AHEAD = 2
 LAG = 2
 WROWS = 16
 FRAME_PARAMS = pltpu.CompilerParams(vmem_limit_bytes=32 << 20)
@@ -161,7 +161,7 @@
     head_dim = width // heads
     a_idx = lax.axis_index("atoms")
     s_idx = lax.axis_index("section")
-    tile = max(count, min(256, total // 4))
+    tile = 256 if total % 256 == 0 else count
     tiles = total // tile
     per_tile = tile // count
     group = max(1, 256 // tile)
@@ -201,21 +201,27 @@
         w, gain, _ = params[b]
         norm = lax.rsqrt(jnp.mean(h[t] * h[t], axis=0, keepdims=True) + 1e-06)
         x = (h[t] * norm * gain[:, :1]).astype(BF16)
-        qkv = dot(w[: 3 * width], x)
-        k = jnp.transpose(qkv[width : 2 * width].astype(BF16))
-        q = (qkv[:width] * scale).astype(BF16)
-        v = qkv[2 * width :].astype(BF16)
+        k = jnp.transpose(dot(w[width : 2 * width], x).astype(BF16))
+        q = dot(w[:width], x).astype(BF16).astype(F32) * scale
+        q_hi = q.astype(BF16)
+        q_lo = (q - q_hi.astype(F32)).astype(BF16)
+        v = None
+        if b + 1 < n_section:
+            v = dot(w[2 * width : 3 * width], x).astype(BF16)
         rhs = []
         for first in range(0, heads, group):
             cols = []
             for hd in range(first, first + group):
-                rows = [q[hd * head_dim : (hd + 1) * head_dim]]
-                if hd > 0:
-                    rows.insert(0, zero_rows(hd * head_dim))
-                if hd < heads - 1:
-                    rows.append(zero_rows((heads - 1 - hd) * head_dim))
+                rows = []
+                for term in (q_hi, q_lo):
+                    if hd > 0:
+                        rows.append(zero_rows(hd * head_dim))
+                    rows.append(term[hd * head_dim : (hd + 1) * head_dim])
+                    if hd < heads - 1:
+                        rows.append(zero_rows((heads - 1 - hd) * head_dim))
                 cols.append(jnp.concatenate(rows, axis=0))
             rhs.append(jnp.concatenate(cols, axis=1))
+        k = jnp.concatenate([k, k], axis=1)
         state[b, t] = rhs, k, v
 
     def score(b, t, jt, g):
@@ -237,14 +243,17 @@
 
     def message(unit, value):
         b, t, jt, g = unit
-        rows = slice(g * group * head_dim, (g + 1) * group * head_dim)
-        lhs = jnp.concatenate([state[b, jt][2][rows], tail[:, span[jt]]], axis=0)
+        lhs, base = tail[:, span[jt]], 0
+        if b + 1 < n_section:
+            base = group * head_dim
+            rows = slice(g * base, (g + 1) * base)
+            lhs = jnp.concatenate([state[b, jt][2][rows], lhs], axis=0)
         res = dot(lhs, value)
         for i in range(group):
             lanes = slice(i * tile, (i + 1) * tile)
             own = (
-                res[i * head_dim : (i + 1) * head_dim, lanes],
-                res[group * head_dim : group * head_dim + 8, lanes],
+                res[base : base + 8, lanes],
+                *([res[i * head_dim : (i + 1) * head_dim, lanes]] if base else []),
             )
             key = b, t, g * group + i
             if key in results:
@@ -255,12 +264,12 @@
         w, _, coef = params[b]
         parts = [results.pop((b, t, hd)) for hd in range(heads)]
         if b + 1 < n_section:
-            msg = jnp.concatenate([part[0] for part in parts], axis=0) * (1.0 / slots)
+            msg = jnp.concatenate([part[1] for part in parts], axis=0) * (1.0 / slots)
             step = dot(w[3 * width :], msg.astype(BF16))
             h[t] = (h[t] + step).astype(BF16).astype(F32)
             project(b + 1, t)
         for hd, part in enumerate(parts):
-            term = coef[:, hd : hd + 1] * part[1]
+            term = coef[:, hd : hd + 1] * part[0]
             force[t] = term if force[t] is None else force[t] + term
 
     last = tiles - 1

time: 32.4 us -> 32 us (0.988)
  Pallas kernels: 12.6 us -> 12.2 us
    pallas_call x1, Pallas kernels: 6.98 us -> 6.61 us  [body(): pl.pallas_call(lambda *refs: frame_kernel(n_section, n_atoms, heads, slot...]
  transfers between devices with their start and end apart: 9 -> 9, of which waited for: 3 -> 3; matrix products, arithmetic and copies ran while one was open for 0% -> 0% of each run, Pallas kernels for 11% -> 12%
where the time goes in v2:
time: 32 us; the launch traced here: 31.7 us
  starting transfers between devices  15.8 us (49%)
  Pallas kernels  12.2 us (38%)
  waiting for transfers between devices  2.96 us (9%)
  between operations  0.74 us (2%)
    ppermute x6, starting transfers between devices, exchange(): lax.ppermute(x, axis, [(i, dest(axis_size, i, r)) for i in range(axis_siz...  13.9 us
    pallas_call x1, Pallas kernels, body(): pl.pallas_call(lambda *refs: frame_kernel(n_section, n_atoms, heads, slot...  6.61 us
    pallas_call x4, Pallas kernels, body(): pl.pallas_call(lambda *refs: slice_kernel(total, *refs), out_shape=shape(...  2.92 us
    ppermute x3, waiting for transfers between devices, joint(): return lax.ppermute(force, ('member', 'atoms'), pairs)  1.96 us
    ppermute x3, starting transfers between devices, joint(): return lax.ppermute(force, ('member', 'atoms'), pairs)  1.89 us
    pallas_call x1, Pallas kernels, body(): pl.pallas_call(lambda *refs: pack_kernel(n_section, *refs), out_shape=[sh...  1.21 us
    ppermute x6, waiting for transfers between devices, exchange(): lax.ppermute(x, axis, [(i, dest(axis_size, i, r)) for i in range(axis_siz...  1 us
    pallas_call x1, Pallas kernels, body(): pl.pallas_call(lambda *refs: pairs_kernel(n_atoms, *refs), out_shape=[sha...  0.77 us
  transfers between devices with their start and end apart: 9, of which 3 were waited for; matrix products, arithmetic and copies ran while one was open for 0% of the time, Pallas kernels for 12%

profile of v2, /device:TPU:0, one launch (start us, length us, event | category | flops | bytes accessed | tf_op | source)
XLA Modules:
  0.0 31.7 jit_solution(7916924631321125578)
XLA Ops:
  0.6 1.2 %pack.1 = (f32[136,128]{1,0:T(8,128)S(1)}, f32[136,128]{1,0:T(8,128)S(1)}, bf16[144,512]{1,0:T(8,128)(2,1)S(1)}) custom-call(f32[3,8,128]{2,1,0:T(8,128)} %bitcast.10, s32[8,128]{1,0:T(8,128)} %refs_1_.1, s32[8,128,128]{2,1,0:T(8,128)} %refs_2_.1, s32[8,128,128]{2,1,0:T(8,128)} %refs_3_.1, bf16[128,384]{1,0:T(8,128)(2,1)} %bitcast.8, ...), custom_call_target="tpu_custom_call" | custom-call | tf_op jit(solution)/shard_map/pack/pallas_call | solution.py:364
  1.9 3.0 %collective-permute-start.3 = (bf16[144,512]{1,0:T(8,128)(2,1)S(1)}, bf16[144,512]{1,0:T(8,128)(2,1)S(1)}, u32[]{:S(2)}, u32[]{:S(2)}) collective-permute-start(bf16[144,512]{1,0:T(8,128)(2,1)S(1)} %get-tuple-element.13.refs_4_), channel_id=1, source_target_pairs={{0,4},{4,0},{8,12},{12,8},{1,5},{5,1},{9,13},{13,9},{2,6},{6,2},{1... | collective-permute-start | bytes 442376 | tf_op jit(solution)/shard_map/ppermute | solution.py:37
  4.9 1.5 %collective-permute-start.4 = (bf16[144,512]{1,0:T(8,128)(2,1)S(1)}, bf16[144,512]{1,0:T(8,128)(2,1)S(1)}, u32[]{:S(2)}, u32[]{:S(2)}) collective-permute-start(bf16[144,512]{1,0:T(8,128)(2,1)S(1)} %get-tuple-element.13.refs_4_), channel_id=1, source_target_pairs={{0,8},{4,12},{8,0},{12,4},{1,9},{5,13},{9,1},{13,5},{2,10},{6,14},... | collective-permute-start | bytes 442376 | tf_op jit(solution)/shard_map/ppermute | solution.py:37
  6.4 0.0 collective-permute-start.5
  6.4 3.0 %collective-permute-start.1 = (f32[136,128]{1,0:T(8,128)S(1)}, f32[136,128]{1,0:T(8,128)S(1)}, u32[]{:S(2)}, u32[]{:S(2)}) collective-permute-start(f32[136,128]{1,0:T(8,128)S(1)} %get-tuple-element.11.refs_0_), channel_id=1, source_target_pairs={{0,2},{1,3},{2,0},{3,1},{4,6},{5,7},{6,4},{7,5},{8,10},{9,11},{10,... | collective-permute-start | bytes 208904 | tf_op jit(solution)/shard_map/ppermute | solution.py:37
  9.5 1.6 %collective-permute-start = (f32[136,128]{1,0:T(8,128)S(1)}, f32[136,128]{1,0:T(8,128)S(1)}, u32[]{:S(2)}, u32[]{:S(2)}) collective-permute-start(f32[136,128]{1,0:T(8,128)S(1)} %get-tuple-element.12), channel_id=1, source_target_pairs={{0,1},{1,0},{2,3},{3,2},{4,5},{5,4},{6,7},{7,6},{8,9},{9,8},{10,11... | collective-permute-start | bytes 208904 | tf_op jit(solution)/shard_map/ppermute | solution.py:37
  11.1 0.9 %collective-permute-done.1.refs_0_.refs_2_ = f32[136,128]{1,0:T(8,128)S(1)} collective-permute-done((f32[136,128]{1,0:T(8,128)S(1)}, f32[136,128]{1,0:T(8,128)S(1)}, u32[]{:S(2)}, u32[]{:S(2)}) %collective-permute-start.1) | collective-permute-done | bytes 69664 | tf_op jit(solution)/shard_map/ppermute | solution.py:37
  12.0 4.7 %collective-permute-start.2 = (f32[136,128]{1,0:T(8,128)S(1)}, f32[136,128]{1,0:T(8,128)S(1)}, u32[]{:S(2)}, u32[]{:S(2)}) collective-permute-start(f32[136,128]{1,0:T(8,128)S(1)} %get-tuple-element.12), channel_id=1, source_target_pairs={{0,3},{1,2},{2,1},{3,0},{4,7},{5,6},{6,5},{7,4},{8,11},{9,10},{10,... | collective-permute-start | bytes 208904 | tf_op jit(solution)/shard_map/ppermute | solution.py:37
  16.7 0.7 %slice.4.refs_4_ = s32[128,128]{1,0:T(8,128)S(1)} custom-call(f32[136,128]{1,0:T(8,128)S(1)} %get-tuple-element.11.refs_0_), custom_call_target="tpu_custom_call" | custom-call | tf_op jit(solution)/shard_map/slice/pallas_call | solution.py:401
  17.4 0.7 %slice.6.refs_6_ = s32[128,128]{1,0:T(8,128)S(1)} custom-call(f32[136,128]{1,0:T(8,128)S(1)} %collective-permute-done.1.refs_0_.refs_2_), custom_call_target="tpu_custom_call" | custom-call | tf_op jit(solution)/shard_map/slice/pallas_call | solution.py:401
  18.1 0.0 collective-permute-done.refs_0_.refs_1_
  18.2 0.7 %slice.5.refs_5_ = s32[128,128]{1,0:T(8,128)S(1)} custom-call(f32[136,128]{1,0:T(8,128)S(1)} %collective-permute-done.refs_0_.refs_1_), custom_call_target="tpu_custom_call" | custom-call | tf_op jit(solution)/shard_map/slice/pallas_call | solution.py:401
  18.9 0.0 copy-start
  18.9 0.1 collective-permute-done.2.refs_0_.refs_3_
  19.0 0.7 %slice.7.refs_7_ = s32[128,128]{1,0:T(8,128)S(1)} custom-call(f32[136,128]{1,0:T(8,128)S(1)} %collective-permute-done.2.refs_0_.refs_3_), custom_call_target="tpu_custom_call" | custom-call | tf_op jit(solution)/shard_map/slice/pallas_call | solution.py:401
  19.7 0.0 copy-done
  19.7 0.8 %pairs.1 = (f32[512,512]{1,0:T(8,128)S(1)}, f32[128,512]{1,0:T(8,128)S(1)}) custom-call(f32[136,128]{1,0:T(8,128)S(1)} %get-tuple-element.11.refs_0_, f32[136,128]{1,0:T(8,128)S(1)} %collective-permute-done.refs_0_.refs_1_, f32[136,128]{1,0:T(8,128)S(1)} %collective-permute-done.1.refs_0_.refs_2_, f32[136,128]{1,0:T(8,128)S(1)} %collective-permute-done.2.refs_0_.refs_3_, ...), custom_call_target="tpu_custom_call" | custom-call | tf_op jit(solution)/shard_map/pairs/pallas_call | solution.py:411
  20.5 0.0 collective-permute-done.3.refs_5_
  20.5 0.0 collective-permute-done.4.refs_6_
  20.5 0.0 collective-permute-done.5.refs_7_
  20.5 6.6 %frame.1.refs_0_ = f32[8,512]{1,0:T(8,128)S(1)} custom-call(f32[136,128]{1,0:T(8,128)S(1)} %get-tuple-element.11.refs_0_, f32[136,128]{1,0:T(8,128)S(1)} %collective-permute-done.refs_0_.refs_1_, f32[136,128]{1,0:T(8,128)S(1)} %collective-permute-done.1.refs_0_.refs_2_, f32[136,128]{1,0:T(8,128)S(1)} %collective-permute-done.2.refs_0_.refs_3_, ...), custom_call_target="tpu_custom_call" | custom-call | tf_op jit(solution)/shard_map/frame/pallas_call | solution.py:420
  27.1 0.1 collective-permute-start.6
  27.2 0.1 collective-permute-start.7
  27.3 1.8 %collective-permute-start.8 = (f32[8,512]{1,0:T(8,128)S(1)}, f32[8,512]{1,0:T(8,128)S(1)}, u32[]{:S(2)}, u32[]{:S(2)}) collective-permute-start(f32[8,512]{1,0:T(8,128)S(1)} %frame.1.refs_0_), channel_id=1, source_target_pairs={{0,17},{1,16},{2,19},{3,18},{16,1},{17,0},{18,3},{19,2},{4,21},{5,... | collective-permute-start | bytes 49160 | tf_op jit(solution)/shard_map/ppermute | solution.py:438
  29.0 0.0 collective-permute-done.6.refs_1_
  29.1 2.0 %collective-permute-done.7.refs_2_ = f32[8,512]{1,0:T(8,128)S(1)} collective-permute-done((f32[8,512]{1,0:T(8,128)S(1)}, f32[8,512]{1,0:T(8,128)S(1)}, u32[]{:S(2)}, u32[]{:S(2)}) %collective-permute-start.7) | collective-permute-done | bytes 16416 | tf_op jit(solution)/shard_map/ppermute | solution.py:438
  31.0 0.0 collective-permute-done.8.refs_3_
  31.0 0.7 %emit.1 = (f32[2,128]{1,0:T(2,128)}, f32[2]{0:T(128)}, f32[3,2,128]{2,1,0:T(2,128)}) custom-call(f32[8,512]{1,0:T(8,128)S(1)} %frame.1.refs_0_, f32[8,512]{1,0:T(8,128)S(1)} %collective-permute-done.6.refs_1_, f32[8,512]{1,0:T(8,128)S(1)} %collective-permute-done.7.refs_2_, f32[8,512]{1,0:T(8,128)S(1)} %collective-permute-done.8.refs_3_), custom_call_target="tpu_custom_call" | custom-call | tf_op jit(solution)/shard_map/emit/pallas_call | solution.py:441
Async XLA Ops:
  1.9 18.6 %collective-permute-start.3 = (bf16[144,512]{1,0:T(8,128)(2,1)S(1)}, bf16[144,512]{1,0:T(8,128)(2,1)S(1)}, u32[]{:S(2)}, u32[]{:S(2)}) collective-permute-start(bf16[144,512]{1,0:T(8,128)(2,1)S(1)} %get-tuple-element.13.refs_4_), channel_id=1, source_target_pairs={{0,4},{4,0},{8,12},{12,8},{1,5},{5,1},{9,13},{13,9},{2,6},{6,2},{1... | collective-permute-start | bytes 442376 | tf_op jit(solution)/shard_map/ppermute | solution.py:37
  4.9 15.6 %collective-permute-start.4 = (bf16[144,512]{1,0:T(8,128)(2,1)S(1)}, bf16[144,512]{1,0:T(8,128)(2,1)S(1)}, u32[]{:S(2)}, u32[]{:S(2)}) collective-permute-start(bf16[144,512]{1,0:T(8,128)(2,1)S(1)} %get-tuple-element.13.refs_4_), channel_id=1, source_target_pairs={{0,8},{4,12},{8,0},{12,4},{1,9},{5,13},{9,1},{13,5},{2,10},{6,14},... | collective-permute-start | bytes 442376 | tf_op jit(solution)/shard_map/ppermute | solution.py:37
  6.4 14.1 %collective-permute-start.5 = (bf16[144,512]{1,0:T(8,128)(2,1)S(1)}, bf16[144,512]{1,0:T(8,128)(2,1)S(1)}, u32[]{:S(2)}, u32[]{:S(2)}) collective-permute-start(bf16[144,512]{1,0:T(8,128)(2,1)S(1)} %get-tuple-element.13.refs_4_), channel_id=1, source_target_pairs={{0,12},{4,8},{8,4},{12,0},{1,13},{5,9},{9,5},{13,1},{2,14},{6,10},... | collective-permute-start | bytes 442376 | tf_op jit(solution)/shard_map/ppermute | solution.py:37
  6.4 5.5 %collective-permute-start.1 = (f32[136,128]{1,0:T(8,128)S(1)}, f32[136,128]{1,0:T(8,128)S(1)}, u32[]{:S(2)}, u32[]{:S(2)}) collective-permute-start(f32[136,128]{1,0:T(8,128)S(1)} %get-tuple-element.11.refs_0_), channel_id=1, source_target_pairs={{0,2},{1,3},{2,0},{3,1},{4,6},{5,7},{6,4},{7,5},{8,10},{9,11},{10,... | collective-permute-start | bytes 208904 | tf_op jit(solution)/shard_map/ppermute | solution.py:37
  9.5 8.7 %collective-permute-start = (f32[136,128]{1,0:T(8,128)S(1)}, f32[136,128]{1,0:T(8,128)S(1)}, u32[]{:S(2)}, u32[]{:S(2)}) collective-permute-start(f32[136,128]{1,0:T(8,128)S(1)} %get-tuple-element.12), channel_id=1, source_target_pairs={{0,1},{1,0},{2,3},{3,2},{4,5},{5,4},{6,7},{7,6},{8,9},{9,8},{10,11... | collective-permute-start | bytes 208904 | tf_op jit(solution)/shard_map/ppermute | solution.py:37
  12.0 7.0 %collective-permute-start.2 = (f32[136,128]{1,0:T(8,128)S(1)}, f32[136,128]{1,0:T(8,128)S(1)}, u32[]{:S(2)}, u32[]{:S(2)}) collective-permute-start(f32[136,128]{1,0:T(8,128)S(1)} %get-tuple-element.12), channel_id=1, source_target_pairs={{0,3},{1,2},{2,1},{3,0},{4,7},{5,6},{6,5},{7,4},{8,11},{9,10},{10,... | collective-permute-start | bytes 208904 | tf_op jit(solution)/shard_map/ppermute | solution.py:37
  18.9 0.8 %copy-start = (bf16[1,128,128]{2,1,0:T(8,128)(2,1)S(1)}, bf16[1,128,128]{2,1,0:T(8,128)(2,1)}, u32[]{:S(2)}) copy-start(bf16[1,128,128]{2,1,0:T(8,128)(2,1)} %param.13) | copy-start | bytes 98308
  27.1 1.9 %collective-permute-start.6 = (f32[8,512]{1,0:T(8,128)S(1)}, f32[8,512]{1,0:T(8,128)S(1)}, u32[]{:S(2)}, u32[]{:S(2)}) collective-permute-start(f32[8,512]{1,0:T(8,128)S(1)} %frame.1.refs_0_), channel_id=1, source_target_pairs={{0,16},{1,17},{2,18},{3,19},{16,0},{17,1},{18,2},{19,3},{4,20},{5,... | collective-permute-start | bytes 49160 | tf_op jit(solution)/shard_map/ppermute | solution.py:438
  27.2 3.8 %collective-permute-start.7 = (f32[8,512]{1,0:T(8,128)S(1)}, f32[8,512]{1,0:T(8,128)S(1)}, u32[]{:S(2)}, u32[]{:S(2)}) collective-permute-start(f32[8,512]{1,0:T(8,128)S(1)} %frame.1.refs_0_), channel_id=1, source_target_pairs={{0,1},{1,0},{2,3},{3,2},{16,17},{17,16},{18,19},{19,18},{4,5},{5,4... | collective-permute-start | bytes 49160 | tf_op jit(solution)/shard_map/ppermute | solution.py:438
  27.3 3.7 %collective-permute-start.8 = (f32[8,512]{1,0:T(8,128)S(1)}, f32[8,512]{1,0:T(8,128)S(1)}, u32[]{:S(2)}, u32[]{:S(2)}) collective-permute-start(f32[8,512]{1,0:T(8,128)S(1)} %frame.1.refs_0_), channel_id=1, source_target_pairs={{0,17},{1,16},{2,19},{3,18},{16,1},{17,0},{18,3},{19,2},{4,21},{5,... | collective-permute-start | bytes 49160 | tf_op jit(solution)/shard_map/ppermute | solution.py:438

commit v3 on v2

--- a/solution.py
+++ b/solution.py
@@ -12,6 +12,7 @@
 EXTRA = 8
 NIBBLES = 8
 AHEAD = 2
+UNROLL = 4
 LAG = 2
 WROWS = 16
 FRAME_PARAMS = pltpu.CompilerParams(vmem_limit_bytes=32 << 20)
@@ -99,21 +100,23 @@
     low = total // NIBBLES
     iota = lax.broadcasted_iota(jnp.int32, (low, count), 0)
     cnt_ref[...] = jnp.zeros_like(cnt_ref)
+    unroll = math.gcd(slots // 8, UNROLL)
 
     def chunk(c, carry):
-        eff = list_ref[pl.ds(c * 8, 8), :]
-        hi = jnp.floor((eff + 0.5) * (1.0 / low))
-        lo = jnp.where(eff < 0, -1.0, eff - hi * low).astype(jnp.int32)
-        weight = jnp.left_shift(1, 4 * jnp.maximum(hi, 0.0).astype(jnp.int32))
-        nib = None
-        for s in range(8):
-            one = jnp.where(iota == lo[s : s + 1, :], weight[s : s + 1, :], 0)
-            nib = one if nib is None else nib + one
-        cnt_ref[:low, :] += nib & 0x0F0F0F0F
-        cnt_ref[low:, :] += lax.shift_right_logical(nib, 4) & 0x0F0F0F0F
+        for u in range(unroll):
+            eff = list_ref[pl.ds(c * 8 * unroll + 8 * u, 8), :]
+            hi = jnp.floor((eff + 0.5) * (1.0 / low))
+            lo = jnp.where(eff < 0, -1.0, eff - hi * low).astype(jnp.int32)
+            weight = jnp.left_shift(1, 4 * jnp.maximum(hi, 0.0).astype(jnp.int32))
+            nib = None
+            for s in range(8):
+                one = jnp.where(iota == lo[s : s + 1, :], weight[s : s + 1, :], 0)
+                nib = one if nib is None else nib + one
+            cnt_ref[:low, :] += nib & 0x0F0F0F0F
+            cnt_ref[low:, :] += lax.shift_right_logical(nib, 4) & 0x0F0F0F0F
         return carry
 
-    lax.fori_loop(0, slots // 8, chunk, 0)
+    lax.fori_loop(0, slots // (8 * unroll), chunk, 0)
 
 
 def slice_kernel(total, msg_ref, cnt_ref):

time: 32 us -> 31.8 us (level)
  Pallas kernels: 12.2 us -> 11.5 us
  waiting for transfers between devices: 2.96 us -> 3.44 us
    pallas_call x4, Pallas kernels: 2.92 us -> 2.27 us  [body(): pl.pallas_call(lambda *refs: slice_kernel(total, *refs), out_shape=shape(...]
    ppermute x6, waiting for transfers between devices: 1 us -> 1.48 us  [exchange(): lax.ppermute(x, axis, [(i, dest(axis_size, i, r)) for i in range(axis_siz...]
  transfers between devices with their start and end apart: 9 -> 9, of which waited for: 3 -> 3; matrix products, arithmetic and copies ran while one was open for 0% -> 0% of each run, Pallas kernels for 12% -> 10%
where the time goes in v3:
time: 31.8 us; the launch traced here: 31.5 us
  starting transfers between devices  15.8 us (50%)
  Pallas kernels  11.5 us (36%)
  waiting for transfers between devices  3.44 us (11%)
  between operations  0.74 us (2%)
    ppermute x6, starting transfers between devices, exchange(): lax.ppermute(x, axis, [(i, dest(axis_size, i, r)) for i in range(axis_siz...  13.9 us
    pallas_call x1, Pallas kernels, body(): pl.pallas_call(lambda *refs: frame_kernel(n_section, n_atoms, heads, slot...  6.61 us
    pallas_call x4, Pallas kernels, body(): pl.pallas_call(lambda *refs: slice_kernel(total, *refs), out_shape=shape(...  2.27 us
    ppermute x3, waiting for transfers between devices, joint(): return lax.ppermute(force, ('member', 'atoms'), pairs)  1.96 us
    ppermute x3, starting transfers between devices, joint(): return lax.ppermute(force, ('member', 'atoms'), pairs)  1.89 us
    ppermute x6, waiting for transfers between devices, exchange(): lax.ppermute(x, axis, [(i, dest(axis_size, i, r)) for i in range(axis_siz...  1.48 us
    pallas_call x1, Pallas kernels, body(): pl.pallas_call(lambda *refs: pack_kernel(n_section, *refs), out_shape=[sh...  1.21 us
    pallas_call x1, Pallas kernels, body(): pl.pallas_call(lambda *refs: pairs_kernel(n_atoms, *refs), out_shape=[sha...  0.77 us
  transfers between devices with their start and end apart: 9, of which 3 were waited for; matrix products, arithmetic and copies ran while one was open for 0% of the time, Pallas kernels for 10%

profile of v3, /device:TPU:0, one launch (start us, length us, event | category | flops | bytes accessed | tf_op | source)
XLA Modules:
  0.0 31.5 jit_solution(5374845322712310375)
XLA Ops:
  0.6 1.2 %pack.1 = (f32[136,128]{1,0:T(8,128)S(1)}, f32[136,128]{1,0:T(8,128)S(1)}, bf16[144,512]{1,0:T(8,128)(2,1)S(1)}) custom-call(f32[3,8,128]{2,1,0:T(8,128)} %bitcast.10, s32[8,128]{1,0:T(8,128)} %refs_1_.1, s32[8,128,128]{2,1,0:T(8,128)} %refs_2_.1, s32[8,128,128]{2,1,0:T(8,128)} %refs_3_.1, bf16[128,384]{1,0:T(8,128)(2,1)} %bitcast.8, ...), custom_call_target="tpu_custom_call" | custom-call | tf_op jit(solution)/shard_map/pack/pallas_call | solution.py:367
  1.9 3.0 %collective-permute-start.3 = (bf16[144,512]{1,0:T(8,128)(2,1)S(1)}, bf16[144,512]{1,0:T(8,128)(2,1)S(1)}, u32[]{:S(2)}, u32[]{:S(2)}) collective-permute-start(bf16[144,512]{1,0:T(8,128)(2,1)S(1)} %get-tuple-element.13.refs_4_), channel_id=1, source_target_pairs={{0,4},{4,0},{8,12},{12,8},{1,5},{5,1},{9,13},{13,9},{2,6},{6,2},{1... | collective-permute-start | bytes 442376 | tf_op jit(solution)/shard_map/ppermute | solution.py:38
  4.9 1.5 %collective-permute-start.4 = (bf16[144,512]{1,0:T(8,128)(2,1)S(1)}, bf16[144,512]{1,0:T(8,128)(2,1)S(1)}, u32[]{:S(2)}, u32[]{:S(2)}) collective-permute-start(bf16[144,512]{1,0:T(8,128)(2,1)S(1)} %get-tuple-element.13.refs_4_), channel_id=1, source_target_pairs={{0,8},{4,12},{8,0},{12,4},{1,9},{5,13},{9,1},{13,5},{2,10},{6,14},... | collective-permute-start | bytes 442376 | tf_op jit(solution)/shard_map/ppermute | solution.py:38
  6.4 0.0 collective-permute-start.5
  6.4 3.0 %collective-permute-start.1 = (f32[136,128]{1,0:T(8,128)S(1)}, f32[136,128]{1,0:T(8,128)S(1)}, u32[]{:S(2)}, u32[]{:S(2)}) collective-permute-start(f32[136,128]{1,0:T(8,128)S(1)} %get-tuple-element.11.refs_0_), channel_id=1, source_target_pairs={{0,2},{1,3},{2,0},{3,1},{4,6},{5,7},{6,4},{7,5},{8,10},{9,11},{10,... | collective-permute-start | bytes 208904 | tf_op jit(solution)/shard_map/ppermute | solution.py:38
  9.5 1.6 %collective-permute-start = (f32[136,128]{1,0:T(8,128)S(1)}, f32[136,128]{1,0:T(8,128)S(1)}, u32[]{:S(2)}, u32[]{:S(2)}) collective-permute-start(f32[136,128]{1,0:T(8,128)S(1)} %get-tuple-element.12), channel_id=1, source_target_pairs={{0,1},{1,0},{2,3},{3,2},{4,5},{5,4},{6,7},{7,6},{8,9},{9,8},{10,11... | collective-permute-start | bytes 208904 | tf_op jit(solution)/shard_map/ppermute | solution.py:38
  11.1 0.9 %collective-permute-done.1.refs_0_.refs_2_ = f32[136,128]{1,0:T(8,128)S(1)} collective-permute-done((f32[136,128]{1,0:T(8,128)S(1)}, f32[136,128]{1,0:T(8,128)S(1)}, u32[]{:S(2)}, u32[]{:S(2)}) %collective-permute-start.1) | collective-permute-done | bytes 69664 | tf_op jit(solution)/shard_map/ppermute | solution.py:38
  12.0 4.7 %collective-permute-start.2 = (f32[136,128]{1,0:T(8,128)S(1)}, f32[136,128]{1,0:T(8,128)S(1)}, u32[]{:S(2)}, u32[]{:S(2)}) collective-permute-start(f32[136,128]{1,0:T(8,128)S(1)} %get-tuple-element.12), channel_id=1, source_target_pairs={{0,3},{1,2},{2,1},{3,0},{4,7},{5,6},{6,5},{7,4},{8,11},{9,10},{10,... | collective-permute-start | bytes 208904 | tf_op jit(solution)/shard_map/ppermute | solution.py:38
  16.7 0.6 %slice.4.refs_4_ = s32[128,128]{1,0:T(8,128)S(1)} custom-call(f32[136,128]{1,0:T(8,128)S(1)} %get-tuple-element.11.refs_0_), custom_call_target="tpu_custom_call" | custom-call | tf_op jit(solution)/shard_map/slice/pallas_call | solution.py:404
  17.3 0.6 %slice.6.refs_6_ = s32[128,128]{1,0:T(8,128)S(1)} custom-call(f32[136,128]{1,0:T(8,128)S(1)} %collective-permute-done.1.refs_0_.refs_2_), custom_call_target="tpu_custom_call" | custom-call | tf_op jit(solution)/shard_map/slice/pallas_call | solution.py:404
  17.8 0.0 collective-permute-done.refs_0_.refs_1_
  17.8 0.6 %slice.5.refs_5_ = s32[128,128]{1,0:T(8,128)S(1)} custom-call(f32[136,128]{1,0:T(8,128)S(1)} %collective-permute-done.refs_0_.refs_1_), custom_call_target="tpu_custom_call" | custom-call | tf_op jit(solution)/shard_map/slice/pallas_call | solution.py:404
  18.4 0.0 copy-start
  18.4 0.5 %collective-permute-done.2.refs_0_.refs_3_ = f32[136,128]{1,0:T(8,128)S(1)} collective-permute-done((f32[136,128]{1,0:T(8,128)S(1)}, f32[136,128]{1,0:T(8,128)S(1)}, u32[]{:S(2)}, u32[]{:S(2)}) %collective-permute-start.2) | collective-permute-done | bytes 69664 | tf_op jit(solution)/shard_map/ppermute | solution.py:38
  19.0 0.6 %slice.7.refs_7_ = s32[128,128]{1,0:T(8,128)S(1)} custom-call(f32[136,128]{1,0:T(8,128)S(1)} %collective-permute-done.2.refs_0_.refs_3_), custom_call_target="tpu_custom_call" | custom-call | tf_op jit(solution)/shard_map/slice/pallas_call | solution.py:404
  19.5 0.0 copy-done
  19.6 0.8 %pairs.1 = (f32[512,512]{1,0:T(8,128)S(1)}, f32[128,512]{1,0:T(8,128)S(1)}) custom-call(f32[136,128]{1,0:T(8,128)S(1)} %get-tuple-element.11.refs_0_, f32[136,128]{1,0:T(8,128)S(1)} %collective-permute-done.refs_0_.refs_1_, f32[136,128]{1,0:T(8,128)S(1)} %collective-permute-done.1.refs_0_.refs_2_, f32[136,128]{1,0:T(8,128)S(1)} %collective-permute-done.2.refs_0_.refs_3_, ...), custom_call_target="tpu_custom_call" | custom-call | tf_op jit(solution)/shard_map/pairs/pallas_call | solution.py:414
  20.3 0.0 collective-permute-done.3.refs_5_
  20.3 0.0 collective-permute-done.4.refs_6_
  20.3 0.0 collective-permute-done.5.refs_7_
  20.4 6.6 %frame.1.refs_0_ = f32[8,512]{1,0:T(8,128)S(1)} custom-call(f32[136,128]{1,0:T(8,128)S(1)} %get-tuple-element.11.refs_0_, f32[136,128]{1,0:T(8,128)S(1)} %collective-permute-done.refs_0_.refs_1_, f32[136,128]{1,0:T(8,128)S(1)} %collective-permute-done.1.refs_0_.refs_2_, f32[136,128]{1,0:T(8,128)S(1)} %collective-permute-done.2.refs_0_.refs_3_, ...), custom_call_target="tpu_custom_call" | custom-call | tf_op jit(solution)/shard_map/frame/pallas_call | solution.py:423
  27.0 0.1 collective-permute-start.6
  27.0 0.1 collective-permute-start.7
  27.1 1.8 %collective-permute-start.8 = (f32[8,512]{1,0:T(8,128)S(1)}, f32[8,512]{1,0:T(8,128)S(1)}, u32[]{:S(2)}, u32[]{:S(2)}) collective-permute-start(f32[8,512]{1,0:T(8,128)S(1)} %frame.1.refs_0_), channel_id=1, source_target_pairs={{0,17},{1,16},{2,19},{3,18},{16,1},{17,0},{18,3},{19,2},{4,21},{5,... | collective-permute-start | bytes 49160 | tf_op jit(solution)/shard_map/ppermute | solution.py:441
  28.9 0.0 collective-permute-done.6.refs_1_
  28.9 2.0 %collective-permute-done.7.refs_2_ = f32[8,512]{1,0:T(8,128)S(1)} collective-permute-done((f32[8,512]{1,0:T(8,128)S(1)}, f32[8,512]{1,0:T(8,128)S(1)}, u32[]{:S(2)}, u32[]{:S(2)}) %collective-permute-start.7) | collective-permute-done | bytes 16416 | tf_op jit(solution)/shard_map/ppermute | solution.py:441
  30.8 0.0 collective-permute-done.8.refs_3_
  30.8 0.7 %emit.1 = (f32[2,128]{1,0:T(2,128)}, f32[2]{0:T(128)}, f32[3,2,128]{2,1,0:T(2,128)}) custom-call(f32[8,512]{1,0:T(8,128)S(1)} %frame.1.refs_0_, f32[8,512]{1,0:T(8,128)S(1)} %collective-permute-done.6.refs_1_, f32[8,512]{1,0:T(8,128)S(1)} %collective-permute-done.7.refs_2_, f32[8,512]{1,0:T(8,128)S(1)} %collective-permute-done.8.refs_3_), custom_call_target="tpu_custom_call" | custom-call | tf_op jit(solution)/shard_map/emit/pallas_call | solution.py:444
Async XLA Ops:
  1.9 18.5 %collective-permute-start.3 = (bf16[144,512]{1,0:T(8,128)(2,1)S(1)}, bf16[144,512]{1,0:T(8,128)(2,1)S(1)}, u32[]{:S(2)}, u32[]{:S(2)}) collective-permute-start(bf16[144,512]{1,0:T(8,128)(2,1)S(1)} %get-tuple-element.13.refs_4_), channel_id=1, source_target_pairs={{0,4},{4,0},{8,12},{12,8},{1,5},{5,1},{9,13},{13,9},{2,6},{6,2},{1... | collective-permute-start | bytes 442376 | tf_op jit(solution)/shard_map/ppermute | solution.py:38
  4.9 15.5 %collective-permute-start.4 = (bf16[144,512]{1,0:T(8,128)(2,1)S(1)}, bf16[144,512]{1,0:T(8,128)(2,1)S(1)}, u32[]{:S(2)}, u32[]{:S(2)}) collective-permute-start(bf16[144,512]{1,0:T(8,128)(2,1)S(1)} %get-tuple-element.13.refs_4_), channel_id=1, source_target_pairs={{0,8},{4,12},{8,0},{12,4},{1,9},{5,13},{9,1},{13,5},{2,10},{6,14},... | collective-permute-start | bytes 442376 | tf_op jit(solution)/shard_map/ppermute | solution.py:38
  6.4 13.9 %collective-permute-start.5 = (bf16[144,512]{1,0:T(8,128)(2,1)S(1)}, bf16[144,512]{1,0:T(8,128)(2,1)S(1)}, u32[]{:S(2)}, u32[]{:S(2)}) collective-permute-start(bf16[144,512]{1,0:T(8,128)(2,1)S(1)} %get-tuple-element.13.refs_4_), channel_id=1, source_target_pairs={{0,12},{4,8},{8,4},{12,0},{1,13},{5,9},{9,5},{13,1},{2,14},{6,10},... | collective-permute-start | bytes 442376 | tf_op jit(solution)/shard_map/ppermute | solution.py:38
  6.4 5.5 %collective-permute-start.1 = (f32[136,128]{1,0:T(8,128)S(1)}, f32[136,128]{1,0:T(8,128)S(1)}, u32[]{:S(2)}, u32[]{:S(2)}) collective-permute-start(f32[136,128]{1,0:T(8,128)S(1)} %get-tuple-element.11.refs_0_), channel_id=1, source_target_pairs={{0,2},{1,3},{2,0},{3,1},{4,6},{5,7},{6,4},{7,5},{8,10},{9,11},{10,... | collective-permute-start | bytes 208904 | tf_op jit(solution)/shard_map/ppermute | solution.py:38
  9.5 8.4 %collective-permute-start = (f32[136,128]{1,0:T(8,128)S(1)}, f32[136,128]{1,0:T(8,128)S(1)}, u32[]{:S(2)}, u32[]{:S(2)}) collective-permute-start(f32[136,128]{1,0:T(8,128)S(1)} %get-tuple-element.12), channel_id=1, source_target_pairs={{0,1},{1,0},{2,3},{3,2},{4,5},{5,4},{6,7},{7,6},{8,9},{9,8},{10,11... | collective-permute-start | bytes 208904 | tf_op jit(solution)/shard_map/ppermute | solution.py:38
  12.0 7.0 %collective-permute-start.2 = (f32[136,128]{1,0:T(8,128)S(1)}, f32[136,128]{1,0:T(8,128)S(1)}, u32[]{:S(2)}, u32[]{:S(2)}) collective-permute-start(f32[136,128]{1,0:T(8,128)S(1)} %get-tuple-element.12), channel_id=1, source_target_pairs={{0,3},{1,2},{2,1},{3,0},{4,7},{5,6},{6,5},{7,4},{8,11},{9,10},{10,... | collective-permute-start | bytes 208904 | tf_op jit(solution)/shard_map/ppermute | solution.py:38
  18.4 1.1 %copy-start = (bf16[1,128,128]{2,1,0:T(8,128)(2,1)S(1)}, bf16[1,128,128]{2,1,0:T(8,128)(2,1)}, u32[]{:S(2)}) copy-start(bf16[1,128,128]{2,1,0:T(8,128)(2,1)} %param.13) | copy-start | bytes 98308
  27.0 1.9 %collective-permute-start.6 = (f32[8,512]{1,0:T(8,128)S(1)}, f32[8,512]{1,0:T(8,128)S(1)}, u32[]{:S(2)}, u32[]{:S(2)}) collective-permute-start(f32[8,512]{1,0:T(8,128)S(1)} %frame.1.refs_0_), channel_id=1, source_target_pairs={{0,16},{1,17},{2,18},{3,19},{16,0},{17,1},{18,2},{19,3},{4,20},{5,... | collective-permute-start | bytes 49160 | tf_op jit(solution)/shard_map/ppermute | solution.py:441
  27.0 3.8 %collective-permute-start.7 = (f32[8,512]{1,0:T(8,128)S(1)}, f32[8,512]{1,0:T(8,128)S(1)}, u32[]{:S(2)}, u32[]{:S(2)}) collective-permute-start(f32[8,512]{1,0:T(8,128)S(1)} %frame.1.refs_0_), channel_id=1, source_target_pairs={{0,1},{1,0},{2,3},{3,2},{16,17},{17,16},{18,19},{19,18},{4,5},{5,4... | collective-permute-start | bytes 49160 | tf_op jit(solution)/shard_map/ppermute | solution.py:441
  27.1 3.7 %collective-permute-start.8 = (f32[8,512]{1,0:T(8,128)S(1)}, f32[8,512]{1,0:T(8,128)S(1)}, u32[]{:S(2)}, u32[]{:S(2)}) collective-permute-start(f32[8,512]{1,0:T(8,128)S(1)} %frame.1.refs_0_), channel_id=1, source_target_pairs={{0,17},{1,16},{2,19},{3,18},{16,1},{17,0},{18,3},{19,2},{4,21},{5,... | collective-permute-start | bytes 49160 | tf_op jit(solution)/shard_map/ppermute | solution.py:441
